TPU v7x, 256 devices: a 8x8x2 block of a 8x8x16 slice. The times are simulated.
256 devices in a mesh: grp: 2 (over z), slab: 128 (over y, x, core).
Axes of the slice: x: 8, y: 8, z: 2, core: 2. Of those that a mesh axis runs over, the one named last changes fastest.
The devices are a block of a 8x8x16 slice.
Arguments:
- volume: bfloat16 [512, 1024, 1024], P(('grp', 'slab')), parts along dimension 0, may hold values from -60 to 60
- plane_shift: int32 [4, 256], P('grp', 'slab'), parts along dimension 0, may hold values from -64 to 64
- plane_weight: float32 [4, 256], P('grp', 'slab'), parts along dimension 0, may hold values from 0 to 1
- column_left: int32 [4, 1024], P('grp'), parts along dimension 0, may hold values from 0 to 1022
- column_weight: float32 [4, 1024], P('grp'), parts along dimension 0, may hold values from 0 to 1
- window_center: int32 [4, 2], P('grp'), parts along dimension 0, may hold values from -200 to 199
- tilt_owner: int32 [256], P('grp'), parts along dimension 0, may hold values from 0 to 127, each once
- reference_band: float32 [256, 2, 128, 128], P(('grp', 'slab')), parts along dimension 0, may hold values from -6 to 6
Outputs:
- correlation: float32 [4, 128, 128], P('grp', 'slab'), parts along dimension 0
- peaks: float32 [4], P('grp'), parts along dimension 0
There are 2 independent parts, one for each index of `grp`. A program takes and returns all parts, laid end to end along the dimension named above; each array names one. Nothing has to cross between parts.
Inputs may be any that keep to these rules, and one draw needn't show every extreme that they name: `tilt_owner`: the first 2 entries name the owners of the tilts, one slab index each.
All inputs are finite; a program needn't handle non-finite values.
Results may differ from a plain program's by a relative error of at most 0.0003.
Values sent between devices are 32-bit elements; how exact they have to be, the bound alone decides.
No kernel may reach another device: no remote copies, remote signals or barrier semaphores. Data moves between devices by JAX's collectives and lax.ppermute only.
A program may use at most 128 MiB of HBM per device.

v0:
```python
import math

import jax
import jax.numpy as jnp
from jax import lax
from jax.sharding import PartitionSpec as P

Y = 1024
X = 1024
BAND = 128
WIN_COLS = 128
TILTS = 2
WIN_ROWS_DEV = 1


def together(arrays, axis):
    ends = [0]
    for a in arrays:
        ends.append(ends[-1] + a.size)
    total = lax.psum(jnp.concatenate([a.ravel() for a in arrays]), axis)
    return tuple((total[b:e].reshape(a.shape) for a, b, e in zip(arrays, ends, ends[1:])))


def phase_pair(left_ints, right_ints, length):
    product = left_ints[:, None] * right_ints[None, :] % length
    angle = product.astype(jnp.float32) * (2.0 * math.pi / length)
    return (jnp.cos(angle), jnp.sin(angle))


def matmul(first, second):
    return jnp.dot(
        first, second, precision=lax.Precision.HIGHEST, preferred_element_type=jnp.float32
    )


def reproject(volume, shifts, weights, left_cols, right_share, row_count):
    grid_width = volume.shape[2]
    margin = grid_width // 16 + 1
    padded_all = jnp.pad(volume, ((0, 0), (0, 0), (margin, margin)))
    summed = jnp.zeros((row_count, grid_width), jnp.float32)
    for plane_no in range(volume.shape[0]):
        padded = padded_all[plane_no]
        near_cells = lax.dynamic_slice_in_dim(
            padded, margin - shifts[plane_no], grid_width, 1
        ).astype(jnp.float32)
        far_cells = lax.dynamic_slice_in_dim(
            padded, margin - shifts[plane_no] - 1, grid_width, 1
        ).astype(jnp.float32)
        summed = summed + (1.0 - weights[plane_no]) * near_cells + weights[plane_no] * far_cells
    left_values = jnp.take(summed, left_cols, axis=1)
    right_values = jnp.take(summed, left_cols + 1, axis=1)
    return (1.0 - right_share) * left_values + right_share * right_values


def band_part(projected):
    row_count, grid_width = projected.shape
    freq_cols = jnp.arange(BAND, dtype=jnp.int32)
    freq_rows = freq_cols - BAND // 2
    col_cos, col_sin = phase_pair(jnp.arange(grid_width, dtype=jnp.int32), freq_cols, grid_width)
    real_half = matmul(projected, col_cos)
    imag_half = -matmul(projected, col_sin)
    row_ids = jnp.arange(row_count, dtype=jnp.int32)
    row_cos, row_sin = phase_pair(freq_rows, row_ids, Y)
    spec_real = matmul(row_cos, real_half) + matmul(row_sin, imag_half)
    spec_imag = matmul(row_cos, imag_half) - matmul(row_sin, real_half)
    return jnp.stack([spec_real, spec_imag])


def correlate(spectrum, owned, center, row_ids, total_rows):
    spec_real, spec_imag = (spectrum[0], spectrum[1])
    ref_real, ref_imag = (owned[0], owned[1])
    cross_real = spec_real * ref_real + spec_imag * ref_imag
    cross_imag = spec_imag * ref_real - spec_real * ref_imag
    energy_spec = jnp.mean(spec_real * spec_real + spec_imag * spec_imag) + 1e-06
    energy_ref = jnp.mean(ref_real * ref_real + ref_imag * ref_imag) + 1e-06
    freq_cols = jnp.arange(BAND, dtype=jnp.int32)
    freq_rows = freq_cols - BAND // 2
    offsets_y = center[0] + row_ids - total_rows // 2
    offsets_x = center[1] + jnp.arange(WIN_COLS, dtype=jnp.int32) - WIN_COLS // 2
    row_cos, row_sin = phase_pair(offsets_y, freq_rows, Y)
    col_cos, col_sin = phase_pair(freq_cols, offsets_x, X)
    half_real = matmul(row_cos, cross_real) - matmul(row_sin, cross_imag)
    half_imag = matmul(row_cos, cross_imag) + matmul(row_sin, cross_real)
    return (matmul(half_real, col_cos) - matmul(half_imag, col_sin)) / (
        BAND * jnp.sqrt(energy_spec * energy_ref)
    )


def per_device(
    volume,
    plane_shift,
    plane_weight,
    column_left,
    column_weight,
    window_center,
    tilt_owner,
    reference_band,
):
    devices = lax.axis_size("slab")
    position = lax.axis_index("slab")
    partials = []
    for which in range(TILTS):

        def rows_term(first_row, row_count, which=which):
            return reproject(
                volume,
                plane_shift[which],
                plane_weight[which],
                column_left[which],
                column_weight[which],
                row_count,
            )

        partials.append(band_part(rows_term(0, Y)))
    stacked = jnp.stack(partials)
    mine = reference_band[0]
    owned_all = jnp.stack(
        [jnp.where(tilt_owner[which] == position, mine, 0.0) for which in range(TILTS)]
    )
    spectra, references = together((stacked, owned_all), "slab")
    total_rows = WIN_ROWS_DEV * devices
    outputs = []
    maxima = []
    row_ids = jnp.arange(total_rows, dtype=jnp.int32)
    for which in range(TILTS):
        corr = correlate(
            spectra[which], references[which], window_center[which], row_ids, total_rows
        )
        outputs.append(lax.dynamic_slice_in_dim(corr, position * WIN_ROWS_DEV, WIN_ROWS_DEV, 0))
        maxima.append(jnp.max(corr))
    peaks = jnp.stack(maxima)
    return (jnp.stack(outputs), peaks)


def solution(mesh):
    placed = (
        P(("grp", "slab"), None, None),
        P("grp", "slab"),
        P("grp", "slab"),
        P("grp", None),
        P("grp", None),
        P("grp", None),
        P("grp"),
        P(("grp", "slab"), None, None, None),
    )
    return jax.shard_map(
        per_device,
        mesh=mesh,
        in_specs=placed,
        out_specs=(P("grp", "slab", None), P("grp")),
        check_vma=False,
    )
```

profile of v0, /device:TPU:513, one launch (start us, length us, event | category | flops | bytes accessed | tf_op | source)
XLA Modules:
  0.0 393.0 jit_solution(5019161472530117699)
XLA Ops:
  23.9 6.2 %copy.10 = bf16[2,1024,1024]{1,2,0:T(8,128)(2,1)} copy(bf16[2,1024,1024]{2,1,0:T(8,128)(2,1)} %param.10) | data formatting | bytes 8388608 | tf_op args[0]
  30.1 5.0 %pad_slice_fusion.1 = (bf16[1,1024,1154]{1,2,0:T(8,128)(2,1)S(1)}, bf16[1,1024,1154]{1,2,0:T(8,128)(2,1)}) fusion(bf16[2,1024,1024]{1,2,0:T(8,128)(2,1)} %copy.10), kind=kLoop, calls=%fused_computation.5 | loop fusion | bytes 8921088 | tf_op jit(solution)/shard_map/slice | solution.py:42
  35.1 12.6 %add_bitcast_fusion.1 = (f32[1024,1024]{0,1:T(8,128)}, f32[1024,1024]{0,1:T(8,128)}) fusion(bf16[1,1024,1154]{1,2,0:T(8,128)(2,1)} %get-tuple-element.10, s32[]{:T(128)S(6)} %select_n.111, f32[]{:T(128)} %bitcast.8, s32[]{:T(128)S(6)} %select_n.110, f32[]{:T(128)S(6)} %sub.142, bf16[1,1024,1154]{1,2,0:T(8,128)(2,1)S(1)} %get-tuple-element.9, ...), kind=kLoop, calls=%fused_computation.13 | loop fusion | flops 23068672 | bytes 25165888 | tf_op jit(solution)/shard_map/add | solution.py:49
  47.8 8.6 %gather_fusion = f32[1024,1024]{1,0:T(8,128)} fusion(f32[1024,1024]{0,1:T(8,128)} %get-tuple-element.7, s32[1024]{0:T(1024)S(1)} %get-tuple-element.25), kind=kCustom, calls=%fused_computation.clone | custom fusion | bytes 8392704 | tf_op jit(solution)/shard_map/jit(_take)/gather | solution.py:50
  56.4 8.6 %gather_fusion.1 = f32[1024,1024]{1,0:T(8,128)} fusion(f32[1024,1024]{0,1:T(8,128)} %get-tuple-element.7, s32[1024]{0:T(1024)S(1)} %get-tuple-element.26), kind=kCustom, calls=%fused_computation.1.clone | custom fusion | bytes 8392704 | tf_op jit(solution)/shard_map/jit(_take)/gather | solution.py:51
  65.0 4.4 %fusion.1 = f32[1024,1024]{0,1:T(8,128)S(1)} fusion(f32[1024,1024]{1,0:T(8,128)} %gather_fusion.1, f32[1024,1024]{1,0:T(8,128)} %gather_fusion, f32[1024]{0:T(1024)S(1)} %bitcast.117, f32[1024]{0:T(1024)S(1)} %bitcast.116, pred[1024]{0:T(1024)(128)(4,1)S(1)} %get-tuple-element.49, pred[1024]{0:T(1024)(128)(4,1)S(1)} %get-tuple-element.50), kind=kLoop, calls=%fused_computation.10 | loop fusion | flops 5242880 | bytes 12593152 | tf_op jit(solution)/shard_map/add | solution.py:52
  69.4 8.5 %fusion.24 = f32[1024,128]{1,0:T(8,128)S(1)} fusion(f32[1024,1024]{0,1:T(8,128)S(1)} %fusion.1), kind=kOutput, calls=%fused_computation.56 | convolution fusion | flops 1612447744 | bytes 4718592 | tf_op jit(solution)/shard_map/dot_general | solution.py:31
  77.9 21.3 %convolution_negate_fusion.1 = f32[1024,128]{1,0:T(8,128)S(1)} fusion(f32[1024,1024]{0,1:T(8,128)S(1)} %fusion.1), kind=kOutput, calls=%fused_computation.15 | convolution fusion | flops 1612578816 | bytes 4718592 | tf_op jit(solution)/shard_map/dot_general | solution.py:31
  99.2 8.6 %gather_fusion.2 = f32[1024,1024]{1,0:T(8,128)} fusion(f32[1024,1024]{0,1:T(8,128)} %get-tuple-element.8, s32[1024]{0:T(1024)S(1)} %get-tuple-element.52), kind=kCustom, calls=%fused_computation.2.clone | custom fusion | bytes 8392704 | tf_op jit(solution)/shard_map/jit(_take)/gather | solution.py:50
  107.8 8.6 %gather_fusion.3 = f32[1024,1024]{1,0:T(8,128)} fusion(f32[1024,1024]{0,1:T(8,128)} %get-tuple-element.8, s32[1024]{0:T(1024)S(1)} %get-tuple-element.51), kind=kCustom, calls=%fused_computation.3.clone | custom fusion | bytes 8392704 | tf_op jit(solution)/shard_map/jit(_take)/gather | solution.py:51
  116.4 4.0 %fusion = f32[1024,1024]{0,1:T(8,128)S(1)} fusion(f32[1024,1024]{1,0:T(8,128)} %gather_fusion.3, f32[1024,1024]{1,0:T(8,128)} %gather_fusion.2, f32[1024]{0:T(1024)S(1)} %bitcast.115, f32[1024]{0:T(1024)S(1)} %bitcast.114, pred[1024]{0:T(1024)(128)(4,1)S(1)} %get-tuple-element.28, pred[1024]{0:T(1024)(128)(4,1)S(1)} %get-tuple-element.27), kind=kLoop, calls=%fused_computation.7 | loop fusion | flops 5242880 | bytes 12593152 | tf_op jit(solution)/shard_map/add | solution.py:52
  120.4 8.5 %fusion.22 = f32[1024,128]{1,0:T(8,128)S(1)} fusion(f32[1024,1024]{0,1:T(8,128)S(1)} %fusion), kind=kOutput, calls=%fused_computation.55 | convolution fusion | flops 1612447744 | bytes 4718592 | tf_op jit(solution)/shard_map/dot_general | solution.py:31
  128.9 8.9 %convolution_negate_fusion = f32[1024,128]{1,0:T(8,128)S(1)} fusion(f32[1024,1024]{0,1:T(8,128)S(1)} %fusion), kind=kOutput, calls=%fused_computation.14 | convolution fusion | flops 1612578816 | bytes 4718592 | tf_op jit(solution)/shard_map/dot_general | solution.py:31
  137.9 3.0 fusion.36
  140.9 3.0 fusion.34
  143.9 3.0 fusion.7
  146.9 3.0 fusion.6
  149.9 3.0 fusion.32
  152.9 3.2 fusion.30
  156.1 3.0 fusion.5
  159.1 3.0 fusion.4
  168.2 202.6 %all-reduce.3.cloned.1.call-done = f32[131072]{0:T(1024)} async-done(((f32[131072]{0:T(1024)}), f32[131072]{0:T(1024)}) %all-reduce.3.cloned.1.call-update) | async-done | bytes 524304 | tf_op jit(solution)/shard_map/psum | solution.py:20
  374.0 1.8 add_reduce_fusion.2
  383.5 1.9 pad_maximum_fusion.4
  (45 shorter events, 17.3 us)
Async XLA Ops:
  7.2 363.7 %all-reduce.3.cloned.1.call-start = ((), (), s32[]{:S(2)}) async-start(), calls=%async_computation | async-start | bytes 1048576 | tf_op jit(solution)/shard_map/psum | solution.py:20
  56.4 8.6 %copy-start.1 = (f32[2,1024]{1,0:T(2,128)S(1)}, f32[2,1024]{1,0:T(2,128)}, u32[]{:S(2)}) copy-start(f32[2,1024]{1,0:T(2,128)} %param.14) | copy-start | bytes 24580
  149.9 12.2 %copy-start.3 = (s32[128]{0:T(128)S(1)}, s32[128]{0:T(128)}, u32[]{:S(2)}) copy-start(s32[128]{0:T(128)} %param.16) | copy-start | bytes 1540
  152.9 11.2 %copy-start = (f32[1,2,128,128]{3,2,1,0:T(8,128)S(1)}, f32[1,2,128,128]{3,2,1,0:T(8,128)}, u32[]{:S(2)}) copy-start(f32[1,2,128,128]{3,2,1,0:T(8,128)} %param.17) | copy-start | bytes 393220
  156.1 9.0 %copy-start.2 = (s32[2,2]{1,0:T(2,128)S(1)}, s32[2,2]{1,0:T(2,128)}, u32[]{:S(2)}) copy-start(s32[2,2]{1,0:T(2,128)} %param.15) | copy-start | bytes 52
Sparse Core Ops, SparseCore 0:
  165.1 205.6 all-reduce.2
where the time goes:
time: 400 us; the launch traced here: 393 us
  waiting for transfers between devices  203 us (51%)
  matrix products  78.4 us (20%)
  local copies, waits for them, and re-layouts  50.6 us (13%)
  between operations  31.4 us (8%)
  other arithmetic  29.9 us (7%)
    psum x1, waiting for transfers between devices, together(): total = lax.psum(jnp.concatenate([a.ravel() for a in arrays]), axis)  203 us
    dot_general x24, matrix products, matmul(): jnp.dot(first, second, precision=lax.Precision.HIGHEST, preferred_element...  78.4 us
    gather x2, local copies, waits for them, and re-layouts, reproject(): right_values = jnp.take(summed, left_cols + 1, axis=1)  17.2 us
    gather x2, local copies, waits for them, and re-layouts, reproject(): left_values = jnp.take(summed, left_cols, axis=1)  17.2 us
    add x1, other arithmetic, reproject(): summed + (1.0 - weights[plane_no]) * near_cells  12.6 us
    add x2, other arithmetic, reproject(): return (1.0 - right_share) * left_values + right_share * right_values  8.41 us
  transfers between devices with their start and end apart: 1, of which 1 were waited for; matrix products, arithmetic and copies ran while one was open for 1% of the time, Pallas kernels for 0%

commit v1 on v0

v1 whole, which is shorter than its diff:
```python
import numpy as np

import jax
import jax.numpy as jnp
from jax import lax
from jax.experimental import pallas as pl
from jax.experimental.pallas import tpu as pltpu
from jax.sharding import Mesh, PartitionSpec as P
import ml_dtypes

BAND = 128
HALF = BAND // 2
WIN = 128
TILTS = 2
INNER = 16
PAIRS = HALF // INNER
ROWS = 136
LANES = 128
CH_IN = 12 * PAIRS
CH_MID = 16 * PAIRS
CH_OUT = 24


def split(table):
    table = np.asarray(table, np.float32)
    high = table.astype(ml_dtypes.bfloat16)
    low = (table - high.astype(np.float32)).astype(ml_dtypes.bfloat16)
    return high, low


def turns(a, b, length):
    angle = (a[:, None].astype(np.int64) * b[None, :]) % length * (2.0 * np.pi / length)
    return np.cos(angle), np.sin(angle)


def row_table(length):
    c, s = turns(np.arange(HALF + 1), np.arange(length), length)
    out = np.zeros((ROWS, length))
    out[:HALF] = c[:HALF]
    out[HALF] = c[HALF]
    out[HALF + 1 : BAND] = s[1:HALF]
    out[BAND] = s[HALF]
    high, low = split(out)
    return np.concatenate([high, low])


def column_table(length):
    c, s = turns(np.arange(length), np.arange(BAND), length)
    high, low = split(np.concatenate([c, s], 1))
    return np.stack([high, low])


def window_column_table(length):
    c, s = turns(np.arange(BAND), np.arange(WIN) - WIN // 2, length)
    high, low = split(np.concatenate([c, -s], 0))
    return np.stack([high, low])


def window_row_table(length):
    c, s = turns(np.arange(WIN) - WIN // 2, np.arange(HALF + 1), length)
    out = np.zeros((TILTS, WIN, INNER, CH_OUT))
    for t in range(TILTS):
        for k in range(INNER):
            for r in range(PAIRS):
                p = k * PAIRS + r
                out[t, :, k, 2 * PAIRS * t + r] = c[:, p]
                out[t, :, k, 2 * PAIRS * t + PAIRS + r] = -s[:, p] if p else c[:, HALF]
        out[t, :, 0, 4 * PAIRS + t] = s[:, HALF]
    high, low = split(out.reshape(TILTS * WIN, INNER * CH_OUT))
    return np.stack([high, low])


def dot(a, b):
    return jnp.dot(a, b, preferred_element_type=jnp.float32)


def halves(x):
    high = x.astype(jnp.bfloat16)
    return high, (x - high.astype(jnp.float32)).astype(jnp.bfloat16)


def spectrum_kernel(shift, weight, volume, row_tab, col_tab, left, share, ref, out, rpad, sums, lhs, proj, band):
    planes, height, width = volume.shape
    tiles = width // LANES
    step = 256
    rpad[:, :, :LANES] = jnp.zeros((planes, ROWS, LANES), jnp.float32)
    rpad[:, :, LANES + width :] = jnp.zeros((planes, ROWS, LANES), jnp.float32)
    for z in range(planes):
        for n in range(0, width, step):
            r = dot(row_tab[...], volume[z, :, n : n + step])
            rpad[z, :, LANES + n : LANES + n + step] = r[:ROWS] + r[ROWS:]
    lane = lax.broadcasted_iota(jnp.int32, (8, LANES), 1)
    for t in range(TILTS):

        def shift_rows(g, _, t=t):
            rows = pl.ds(pl.multiple_of(g * 8, 8), 8)
            total = [None] * tiles
            for z in range(planes):
                w = weight[t, z]
                for more, factor in ((0, 1.0 - w), (1, w)):
                    s = shift[t, z] + more
                    off = jnp.where(s < 0, 1, 0)
                    turn = jnp.where(s < 0, s + LANES, s)
                    mask = lane < turn
                    turned = []
                    for j in range(tiles + 1):
                        at = pl.multiple_of((j + off) * LANES, LANES)
                        turned.append(pltpu.roll(rpad[z, rows, pl.ds(at, LANES)], turn, 1))
                    for j in range(tiles):
                        term = factor * jnp.where(mask, turned[j], turned[j + 1])
                        total[j] = term if total[j] is None else total[j] + term
            for j in range(tiles):
                sums[rows, j * LANES : (j + 1) * LANES] = total[j]
            return 0

        lax.fori_loop(0, ROWS // 8, shift_rows, 0)
        here = sums[:ROWS, :]
        sums[ROWS:, :] = pltpu.roll(here, width - 1, 1)
        high, low = halves(sums[...])
        lhs[: 2 * ROWS] = high
        lhs[2 * ROWS :] = low
        place = lax.broadcasted_iota(jnp.int32, (width, step), 0)
        for n in range(0, width, step):
            pick = jnp.where(place == left[t : t + 1, n : n + step], 1.0, 0.0).astype(jnp.bfloat16)
            y = dot(lhs[...], pick)
            y = y[: 2 * ROWS] + y[2 * ROWS :]
            cw = share[t : t + 1, n : n + step]
            proj[t * ROWS : (t + 1) * ROWS, n : n + step] = (1.0 - cw) * y[:ROWS] + cw * y[ROWS:]
    high, low = halves(proj[...])
    band[...] = dot(high, col_tab[0]) + dot(low, col_tab[0]) + dot(high, col_tab[1])
    for t in range(TILTS):
        b = t * ROWS
        row = band[b + HALF : b + HALF + 1, :]
        last = band[b + BAND : b + BAND + 1, :]
        band[b + HALF : b + HALF + 1, :BAND] = row[:, :BAND] + last[:, BAND:]
        band[b + HALF : b + HALF + 1, BAND:] = row[:, BAND:] - last[:, :BAND]
    for k in range(INNER):
        for t in range(TILTS):
            for i, (r0, c0) in enumerate(((0, 0), (0, BAND), (HALF, 0), (HALF, BAND))):
                at = t * ROWS + r0 + k * PAIRS
                to = (4 * t + i) * PAIRS
                out[k, to : to + PAIRS, :] = band[at : at + PAIRS, c0 : c0 + BAND]
        for i in range(2):
            to = (8 + i) * PAIRS
            a = HALF + k * PAIRS
            out[k, to : to + PAIRS, :] = ref[0, i, a : a + PAIRS, :]
            for r in range(PAIRS):
                p = k * PAIRS + r
                a = HALF - p if p else 0
                to = (10 + i) * PAIRS + r
                out[k, to : to + 1, :] = ref[0, i, a : a + 1, :]


def row_sum_kernel(info, got, out):
    n = got.shape[0]
    mine = info[0]
    total = got[0, : 8 * PAIRS, :]
    for s in range(1, n):
        total = total + got[s, : 8 * PAIRS, :]
    refs = []
    for t in range(TILTS):
        owner = info[1 + t]
        piece = got[lax.rem(owner, n), 8 * PAIRS :, :]
        refs.append(jnp.where(lax.div(owner, n) == mine, piece, 0.0))
    for y in range(out.shape[0]):
        out[y, : 8 * PAIRS, :] = total
        for t in range(TILTS):
            out[y, (8 + 4 * t) * PAIRS : (12 + 4 * t) * PAIRS, :] = refs[t]


def cross_kernel(length, info, center, got, tab, out, lhs):
    n = got.shape[0]
    total = got[0]
    for s in range(1, n):
        total = total + got[s]
    k = info[0]
    b = lax.broadcasted_iota(jnp.int32, (PAIRS, BAND), 1)
    p = k * PAIRS + lax.broadcasted_iota(jnp.int32, (PAIRS, BAND), 0)
    zero = p == 0
    lhs[...] = jnp.zeros(lhs.shape, jnp.float32)
    energies = []
    for t in range(TILTS):

        def part(i):
            return total[i * PAIRS : (i + 1) * PAIRS, :]

        cc, cs, sc, ss = (part(4 * t + i) for i in range(4))
        refs = [part(8 + 4 * t + i) for i in range(4)]
        plus = (jnp.where(zero, cc, cc - ss), -jnp.where(zero, cs, cs + sc))
        minus = (jnp.where(zero, sc, cc + ss), -jnp.where(zero, ss, cs - sc))
        crossed = []
        e_spec = e_ref = 0.0
        for (sr, si), (rr, ri), q in ((plus, refs[:2], p), (minus, refs[2:], jnp.where(zero, -HALF, -p))):
            cr = sr * rr + si * ri
            ci = si * rr - sr * ri
            e_spec = e_spec + sr * sr + si * si
            e_ref = e_ref + rr * rr + ri * ri
            angle = ((q * center[t, 0] + b * center[t, 1]) & (length - 1)).astype(jnp.float32) * (2.0 * np.pi / length)
            co, si_ = jnp.cos(angle), jnp.sin(angle)
            crossed.append((cr * co - ci * si_, cr * si_ + ci * co))
        (pr, pi), (mr, mi) = crossed
        at = 2 * PAIRS * t
        lhs[at : at + PAIRS, :BAND] = jnp.where(zero, pr, pr + mr)
        lhs[at : at + PAIRS, BAND:] = jnp.where(zero, pi, pi + mi)
        lhs[at + PAIRS : at + 2 * PAIRS, :BAND] = jnp.where(zero, mr, pi - mi)
        lhs[at + PAIRS : at + 2 * PAIRS, BAND:] = jnp.where(zero, mi, mr - pr)
        extra = 4 * PAIRS + t
        lhs[extra : extra + 1, :BAND] = mi[:1]
        lhs[extra : extra + 1, BAND:] = -mr[:1]
        energies += [jnp.sum(e_spec, 0, keepdims=True), jnp.sum(e_ref, 0, keepdims=True)]
    high, low = halves(lhs[...])
    h = dot(high, tab[0]) + dot(low, tab[0]) + dot(high, tab[1])
    h = h[:CH_OUT]
    for d in range(out.shape[0]):
        out[d] = h
        for i, e in enumerate(energies):
            to = 4 * PAIRS + TILTS + i
            out[d, to : to + 1, :] = e


def window_kernel(info, got, tab, rows, peaks, corr):
    x = got[...].reshape(got.shape[0] * CH_OUT, WIN)
    high, low = halves(x)
    c = dot(tab[0], high) + dot(tab[0], low) + dot(tab[1], high)
    e = jnp.sum(jnp.sum(got[:, 4 * PAIRS + TILTS :, :], 0), 1, keepdims=True)
    for t in range(TILTS):
        spec = e[2 * t : 2 * t + 1] / (BAND * BAND) + 1e-06
        ref = e[2 * t + 1 : 2 * t + 2] / (BAND * BAND) + 1e-06
        mine = c[t * WIN : (t + 1) * WIN] / (BAND * jnp.sqrt(spec * ref))
        corr[t] = mine
        peaks[t] = jnp.max(mine)
        rows[t] = corr[t, pl.ds(info[0], 1), :]


def solution(mesh):
    outer = mesh.shape["slab"] // INNER
    grid = Mesh(
        mesh.devices.reshape(mesh.shape["grp"], outer, INNER), ("grp", "line", "seat")
    )
    slab = ("line", "seat")
    vmem = pl.BlockSpec(memory_space=pltpu.VMEM)
    smem = pl.BlockSpec(memory_space=pltpu.SMEM)
    big = pltpu.CompilerParams(vmem_limit_bytes=48 * 1024 * 1024)

    def per_device(volume, shift, weight, left, share, center, owner, ref):
        planes, height, width = volume.shape
        line = lax.axis_index("line")
        seat = lax.axis_index("seat")
        f32 = jnp.float32
        packed = pl.pallas_call(
            spectrum_kernel,
            out_shape=jax.ShapeDtypeStruct((INNER, CH_IN, BAND), f32),
            in_specs=[smem, smem] + [vmem] * 6,
            out_specs=vmem,
            scratch_shapes=[
                pltpu.VMEM((planes, ROWS, width + 2 * LANES), f32),
                pltpu.VMEM((2 * ROWS, width), f32),
                pltpu.VMEM((4 * ROWS, width), jnp.bfloat16),
                pltpu.VMEM((TILTS * ROWS, width), f32),
                pltpu.VMEM((TILTS * ROWS, 2 * BAND), f32),
            ],
            compiler_params=big,
            name="spectrum",
        )(shift, weight, volume, jnp.asarray(row_table(height)), jnp.asarray(column_table(width)), left, share, ref)
        got = lax.all_to_all(packed, "seat", 0, 0, tiled=True)
        info = jnp.concatenate([line[None], owner[:TILTS]]).astype(jnp.int32)
        summed = pl.pallas_call(
            row_sum_kernel,
            out_shape=jax.ShapeDtypeStruct((outer, CH_MID, BAND), f32),
            in_specs=[smem, vmem],
            out_specs=vmem,
            name="row_sum",
        )(info, got)
        got = lax.all_to_all(summed, "line", 0, 0, tiled=True)

        def cross(*refs):
            cross_kernel(width, *refs)

        piece = pl.pallas_call(
            cross,
            out_shape=jax.ShapeDtypeStruct((INNER, CH_OUT, WIN), f32),
            in_specs=[smem, smem, vmem, vmem],
            out_specs=vmem,
            scratch_shapes=[pltpu.VMEM((32, 2 * BAND), f32)],
            name="cross",
        )(seat[None].astype(jnp.int32), center, got, jnp.asarray(window_column_table(width)))
        got = lax.all_to_all(piece, "seat", 0, 0, tiled=True)
        rows, peaks = pl.pallas_call(
            window_kernel,
            out_shape=[jax.ShapeDtypeStruct((TILTS, 1, WIN), f32), jax.ShapeDtypeStruct((TILTS,), f32)],
            in_specs=[smem, vmem, vmem],
            out_specs=[vmem, smem],
            scratch_shapes=[pltpu.VMEM((TILTS, WIN, WIN), f32)],
            name="window",
        )((line * INNER + seat)[None].astype(jnp.int32), got, jnp.asarray(window_row_table(height)))
        return rows, peaks

    placed = (
        P(("grp",) + slab, None, None),
        P("grp", slab),
        P("grp", slab),
        P("grp", None),
        P("grp", None),
        P("grp", None),
        P("grp"),
        P(("grp",) + slab, None, None, None),
    )
    return jax.shard_map(
        per_device,
        mesh=grid,
        in_specs=placed,
        out_specs=(P("grp", slab, None), P("grp")),
        check_vma=False,
    )
```

time: 400 us -> 95.9 us (0.24); the launches traced: 393 us -> 95.3 us
  waiting for transfers between devices: 203 us -> 36.3 us
  matrix products: 78.4 us -> 0 us
  local copies, waits for them, and re-layouts: 50.6 us -> 8.06 us
  starting transfers between devices: 0.06 us -> 31.1 us
  between operations: 31.4 us -> 0.67 us
  other arithmetic: 29.9 us -> 0.59 us
  Pallas kernels: 0 us -> 18.6 us
    psum x1 -> x0, waiting for transfers between devices: 203 us -> none  [together(): total = lax.psum(jnp.concatenate([a.ravel() for a in arrays]), axis)]
    dot_general x24 -> x0, matrix products: 78.4 us -> none  [matmul(): jnp.dot(first, second, precision=lax.Precision.HIGHEST, preferred_element...]
    all_to_all x0 -> x3, waiting for transfers between devices: none -> 36.3 us  [the longest x1 14.1 us: per_device(): got = lax.all_to_all(packed, 'seat', 0, 0, tiled=True)]
    gather x4 -> x0, local copies, waits for them, and re-layouts: 34.4 us -> none  [the longest x2 17.2 us: reproject(): right_values = jnp.take(summed, left_cols + 1, axis=1)]
    all_to_all x0 -> x3, starting transfers between devices: none -> 31.1 us  [the longest x1 23.8 us: per_device(): got = lax.all_to_all(packed, 'seat', 0, 0, tiled=True)]
    add x3 -> x0, other arithmetic: 21.1 us -> none  [the longest x1 12.6 us: reproject(): summed + (1.0 - weights[plane_no]) * near_cells]
    pallas_call x0 -> x4, Pallas kernels: none -> 18.6 us  [the longest x1 12.7 us: per_device(): pl.pallas_call(spectrum_kernel, out_shape=jax.ShapeDtypeStruct((INNER, CH...]
    slice x6 -> x0, local copies, waits for them, and re-layouts: 9.91 us -> none  [the longest x1 5.02 us: reproject(): padded = padded_all[plane_no]]
  transfers between devices with their start and end apart: 1 -> 3, of which waited for: 1 -> 3; matrix products, arithmetic and copies ran while one was open for 1% -> 1% of each run, Pallas kernels for 0% -> 0%
where the time goes in v1:
time: 95.9 us; the launch traced here: 95.3 us
  waiting for transfers between devices  36.3 us (38%)
  starting transfers between devices  31.1 us (32%)
  Pallas kernels  18.6 us (19%)
  local copies, waits for them, and re-layouts  8.06 us (8%)
    all_to_all x1, starting transfers between devices, per_device(): got = lax.all_to_all(packed, 'seat', 0, 0, tiled=True)  23.8 us
    all_to_all x1, waiting for transfers between devices, per_device(): got = lax.all_to_all(packed, 'seat', 0, 0, tiled=True)  14.1 us
    pallas_call x1, Pallas kernels, per_device(): pl.pallas_call(spectrum_kernel, out_shape=jax.ShapeDtypeStruct((INNER, CH...  12.7 us
    all_to_all x1, waiting for transfers between devices, per_device(): got = lax.all_to_all(summed, 'line', 0, 0, tiled=True)  11.5 us
    all_to_all x1, waiting for transfers between devices, per_device(): got = lax.all_to_all(piece, 'seat', 0, 0, tiled=True)  10.6 us
    unnamed x22, local copies, waits for them, and re-layouts  8.06 us
    all_to_all x1, starting transfers between devices, per_device(): got = lax.all_to_all(piece, 'seat', 0, 0, tiled=True)  3.72 us
    all_to_all x1, starting transfers between devices, per_device(): got = lax.all_to_all(summed, 'line', 0, 0, tiled=True)  3.62 us
  transfers between devices with their start and end apart: 3, of which 3 were waited for; matrix products, arithmetic and copies ran while one was open for 1% of the time, Pallas kernels for 0%

profile of v1, /device:TPU:513, one launch (start us, length us, event | category | flops | bytes accessed | tf_op | source)
XLA Modules:
  0.0 95.3 jit_solution(12586424596096396303)
XLA Ops:
  0.6 0.0 copy-start
  0.6 1.2 %copy-done = bf16[2,1024,256]{2,1,0:T(8,128)(2,1)S(1)} copy-done((bf16[2,1024,256]{2,1,0:T(8,128)(2,1)S(1)}, bf16[2,1024,256]{2,1,0:T(8,128)(2,1)}, u32[]{:S(2)}) %copy-start) | copy-done | bytes 1048600
  1.9 0.0 copy-start.1
  1.9 1.1 %copy-done.1 = bf16[272,1024]{1,0:T(8,128)(2,1)S(1)} copy-done((bf16[272,1024]{1,0:T(8,128)(2,1)S(1)}, bf16[272,1024]{1,0:T(8,128)(2,1)}, u32[]{:S(2)}) %copy-start.1) | copy-done | bytes 557080
  2.9 0.9 copy-done.2
  3.8 0.7 copy-done.3
  4.5 0.7 copy-done.4
  5.2 0.7 copy-done.5
  5.9 0.7 copy-done.6
  6.6 12.7 %spectrum.1 = f32[16,48,128]{2,1,0:T(8,128)} custom-call(s32[2,2]{1,0:T(2,128)S(1)} %copy-done.5, f32[2,2]{1,0:T(2,128)S(1)} %copy-done.6, bf16[2,1024,1024]{2,1,0:T(8,128)(2,1)} %volume.1, bf16[272,1024]{1,0:T(8,128)(2,1)S(1)} %copy-done.1, bf16[2,1024,256]{2,1,0:T(8,128)(2,1)S(1)} %copy-done, s32[2,1024]{1,0:T(2,128)S(1)} %copy-done.3, ...), custom_call_target="tpu_custom_call" | custom-call | tf_op jit(solution)/shard_map/spectrum/pallas_call | solution.py:250
  19.3 23.8 %all-to-all-start = ((f32[16,48,128]{2,1,0:T(8,128)}), f32[16,48,128]{2,1,0:T(8,128)S(1)}, u32[]{:S(2)}, u32[]{:S(2)}) async-start(f32[16,48,128]{2,1,0:T(8,128)} %spectrum.1), calls=%async_computation | async-start | bytes 786432 | tf_op jit(solution)/shard_map/all_to_all | solution.py:265
  43.1 0.0 copy-done.10
  43.1 0.6 pad_add_fusion.info
  43.7 14.1 %all-to-all-done.got = f32[16,48,128]{2,1,0:T(8,128)S(1)} async-done(((f32[16,48,128]{2,1,0:T(8,128)}), f32[16,48,128]{2,1,0:T(8,128)S(1)}, u32[]{:S(2)}, u32[]{:S(2)}) %all-to-all-start) | async-done | bytes 393248 | tf_op jit(solution)/shard_map/all_to_all | solution.py:265
  57.8 0.8 copy-done.7
  58.5 1.7 %row_sum.1 = f32[8,64,128]{2,1,0:T(8,128)} custom-call(s32[3]{0:T(128)} %pad_add_fusion.info, f32[16,48,128]{2,1,0:T(8,128)} %copy-done.7), custom_call_target="tpu_custom_call" | custom-call | tf_op jit(solution)/shard_map/row_sum/pallas_call | solution.py:267
  60.3 3.6 %all-to-all-start.1 = ((f32[8,64,128]{2,1,0:T(8,128)}), f32[8,64,128]{2,1,0:T(8,128)S(1)}, u32[]{:S(2)}, u32[]{:S(2)}) async-start(f32[8,64,128]{2,1,0:T(8,128)} %row_sum.1), calls=%async_computation.1 | async-start | bytes 524288 | tf_op jit(solution)/shard_map/all_to_all | solution.py:274
  63.9 11.5 %all-to-all-done.1.refs_2_ = f32[8,64,128]{2,1,0:T(8,128)S(1)} async-done(((f32[8,64,128]{2,1,0:T(8,128)}), f32[8,64,128]{2,1,0:T(8,128)S(1)}, u32[]{:S(2)}, u32[]{:S(2)}) %all-to-all-start.1) | async-done | bytes 262176 | tf_op jit(solution)/shard_map/all_to_all | solution.py:274
  75.4 0.7 copy-done.8
  76.1 2.0 %cross.1 = f32[16,24,128]{2,1,0:T(8,128)} custom-call(s32[1]{0:T(128)} %bitcast.1.refs_0_, s32[2,2]{1,0:T(2,128)} %refs_1_.1, f32[8,64,128]{2,1,0:T(8,128)} %copy-done.8, bf16[2,256,128]{2,1,0:T(8,128)(2,1)} %constant.21.clone.refs_3_), custom_call_target="tpu_custom_call" | custom-call | tf_op jit(solution)/shard_map/cross/pallas_call | solution.py:279
  78.1 3.7 %all-to-all-start.2 = ((f32[16,24,128]{2,1,0:T(8,128)}), f32[16,24,128]{2,1,0:T(8,128)S(1)}, u32[]{:S(2)}, u32[]{:S(2)}) async-start(f32[16,24,128]{2,1,0:T(8,128)} %cross.1), calls=%async_computation.2 | async-start | bytes 393216 | tf_op jit(solution)/shard_map/all_to_all | solution.py:287
  81.8 10.6 %all-to-all-done.2.got = f32[16,24,128]{2,1,0:T(8,128)S(1)} async-done(((f32[16,24,128]{2,1,0:T(8,128)}), f32[16,24,128]{2,1,0:T(8,128)S(1)}, u32[]{:S(2)}, u32[]{:S(2)}) %all-to-all-start.2) | async-done | bytes 196640 | tf_op jit(solution)/shard_map/all_to_all | solution.py:287
  92.4 0.7 copy-done.9
  93.1 2.2 %window.1 = (f32[2,1,128]{2,1,0:T(1,128)}, f32[2]{0:T(128)}) custom-call(s32[1]{0:T(128)} %bitcast.info, f32[16,24,128]{2,1,0:T(8,128)} %copy-done.9, bf16[2,256,384]{2,1,0:T(8,128)(2,1)} %constant.22.clone.tab), custom_call_target="tpu_custom_call" | custom-call | tf_op jit(solution)/shard_map/window/pallas_call | solution.py:288
  (9 shorter events, 0.0 us)
Async XLA Ops:
  0.6 1.2 %copy-start = (bf16[2,1024,256]{2,1,0:T(8,128)(2,1)S(1)}, bf16[2,1024,256]{2,1,0:T(8,128)(2,1)}, u32[]{:S(2)}) copy-start(bf16[2,1024,256]{2,1,0:T(8,128)(2,1)} %constant.20.clone.col_tab) | copy-start | bytes 3145732
  1.9 1.1 %copy-start.1 = (bf16[272,1024]{1,0:T(8,128)(2,1)S(1)}, bf16[272,1024]{1,0:T(8,128)(2,1)}, u32[]{:S(2)}) copy-start(bf16[272,1024]{1,0:T(8,128)(2,1)} %constant.19.clone.row_tab) | copy-start | bytes 1671172
  2.9 0.9 copy-start.2
  3.8 0.7 copy-start.3
  4.5 0.7 copy-start.4
  5.2 0.7 copy-start.5
  5.9 0.7 copy-start.6
  6.6 36.5 %copy-start.10 = (s32[128]{0:T(128)S(1)}, s32[128]{0:T(128)}, u32[]{:S(2)}) copy-start(s32[128]{0:T(128)} %param.18) | copy-start | bytes 1540
  19.3 38.5 %all-to-all-start = ((f32[16,48,128]{2,1,0:T(8,128)}), f32[16,48,128]{2,1,0:T(8,128)S(1)}, u32[]{:S(2)}, u32[]{:S(2)}) async-start(f32[16,48,128]{2,1,0:T(8,128)} %spectrum.1), calls=%async_computation | async-start | bytes 786432 | tf_op jit(solution)/shard_map/all_to_all | solution.py:265
  57.8 0.8 copy-start.7
  60.3 15.1 %all-to-all-start.1 = ((f32[8,64,128]{2,1,0:T(8,128)}), f32[8,64,128]{2,1,0:T(8,128)S(1)}, u32[]{:S(2)}, u32[]{:S(2)}) async-start(f32[8,64,128]{2,1,0:T(8,128)} %row_sum.1), calls=%async_computation.1 | async-start | bytes 524288 | tf_op jit(solution)/shard_map/all_to_all | solution.py:274
  75.4 0.7 copy-start.8
  78.1 14.4 %all-to-all-start.2 = ((f32[16,24,128]{2,1,0:T(8,128)}), f32[16,24,128]{2,1,0:T(8,128)S(1)}, u32[]{:S(2)}, u32[]{:S(2)}) async-start(f32[16,24,128]{2,1,0:T(8,128)} %cross.1), calls=%async_computation.2 | async-start | bytes 393216 | tf_op jit(solution)/shard_map/all_to_all | solution.py:287
  92.4 0.7 copy-start.9

commit v2 on v1

--- a/solution.py
+++ b/solution.py
@@ -79,41 +79,93 @@
     return high, (x - high.astype(jnp.float32)).astype(jnp.bfloat16)
 
 
-def spectrum_kernel(shift, weight, volume, row_tab, col_tab, left, share, ref, out, rpad, sums, lhs, proj, band):
-    planes, height, width = volume.shape
+def spectrum_kernel(
+    h_shift, h_weight, h_center, h_owner, h_volume, h_row, h_col, h_left, h_share, h_ref, out, aux,
+    shift, weight, center, owner, volume, row_tab, col_tab, left, share, ref,
+    rpad, sums, lhs, proj, band, sem, vsem,
+):
+    planes, height, width = h_volume.shape
     tiles = width // LANES
     step = 256
+    steps = width // step
+
+    def fetch(src, dst, i):
+        copy = pltpu.make_async_copy(src, dst, sem.at[i])
+        copy.start()
+        return copy
+
+    get_row = fetch(h_row, row_tab, 0)
+    blocks = []
+    for z in range(planes):
+        for n in range(steps):
+            i = z * steps + n
+            cols = pl.ds(n * step, step)
+            copy = pltpu.make_async_copy(h_volume.at[z, :, cols], volume.at[i], vsem.at[i])
+            copy.start()
+            blocks.append(copy)
+            if i == 0:
+                get_center = fetch(h_center, center, 1)
+                get_owner = fetch(h_owner, owner, 2)
+                get_shift = fetch(h_shift, shift, 3)
+                get_weight = fetch(h_weight, weight, 4)
+    get_left = fetch(h_left, left, 5)
+    get_share = fetch(h_share, share, 6)
+    get_ref = fetch(h_ref, ref, 7)
+    get_col = fetch(h_col, col_tab, 8)
+
+    line = lax.axis_index("line")
+    seat = lax.axis_index("seat")
     rpad[:, :, :LANES] = jnp.zeros((planes, ROWS, LANES), jnp.float32)
     rpad[:, :, LANES + width :] = jnp.zeros((planes, ROWS, LANES), jnp.float32)
+    get_center.wait()
+    get_owner.wait()
+    row = lax.broadcasted_iota(jnp.int32, (2 * PAIRS, BAND), 0)
+    b = lax.broadcasted_iota(jnp.int32, (2 * PAIRS, BAND), 1)
+    p = seat * PAIRS + (row & (PAIRS - 1))
+    q = jnp.where(row < PAIRS, p, jnp.where(p == 0, -HALF, -p))
+    who = lax.broadcasted_iota(jnp.int32, (INNER, BAND), 0) + line * INNER
+    for t in range(TILTS):
+        turn = (q * center[t, 0] + b * center[t, 1]) & (width - 1)
+        angle = turn.astype(jnp.float32) * (2.0 * np.pi / width)
+        at = t * (4 * PAIRS + INNER)
+        aux[at : at + 2 * PAIRS, :] = jnp.cos(angle)
+        aux[at + 2 * PAIRS : at + 4 * PAIRS, :] = jnp.sin(angle)
+        aux[at + 4 * PAIRS : at + 4 * PAIRS + INNER, :] = jnp.where(who == owner[t], 1.0, 0.0)
+
+    get_row.wait()
     for z in range(planes):
-        for n in range(0, width, step):
-            r = dot(row_tab[...], volume[z, :, n : n + step])
-            rpad[z, :, LANES + n : LANES + n + step] = r[:ROWS] + r[ROWS:]
+        for n in range(steps):
+            i = z * steps + n
+            blocks[i].wait()
+            r = dot(row_tab[...], volume[i])
+            at = LANES + n * step
+            rpad[z, :, at : at + step] = r[:ROWS] + r[ROWS:]
+    get_shift.wait()
+    get_weight.wait()
+    get_left.wait()
+    get_share.wait()
     lane = lax.broadcasted_iota(jnp.int32, (8, LANES), 1)
     for t in range(TILTS):
-
-        def shift_rows(g, _, t=t):
-            rows = pl.ds(pl.multiple_of(g * 8, 8), 8)
+        moves = []
+        for z in range(planes):
+            w = weight[t, z]
+            for more, factor in ((0, 1.0 - w), (1, w)):
+                s = shift[t, z] + more
+                turn = jnp.where(s < 0, s + LANES, s)
+                moves.append((z, jnp.where(s < 0, 1, 0), turn, lane < turn, factor))
+        for g in range(ROWS // 8):
+            rows = slice(g * 8, g * 8 + 8)
             total = [None] * tiles
-            for z in range(planes):
-                w = weight[t, z]
-                for more, factor in ((0, 1.0 - w), (1, w)):
-                    s = shift[t, z] + more
-                    off = jnp.where(s < 0, 1, 0)
-                    turn = jnp.where(s < 0, s + LANES, s)
-                    mask = lane < turn
-                    turned = []
-                    for j in range(tiles + 1):
-                        at = pl.multiple_of((j + off) * LANES, LANES)
-                        turned.append(pltpu.roll(rpad[z, rows, pl.ds(at, LANES)], turn, 1))
-                    for j in range(tiles):
-                        term = factor * jnp.where(mask, turned[j], turned[j + 1])
-                        total[j] = term if total[j] is None else total[j] + term
+            for z, off, turn, mask, factor in moves:
+                turned = []
+                for j in range(tiles + 1):
+                    at = pl.multiple_of((j + off) * LANES, LANES)
+                    turned.append(pltpu.roll(rpad[z, rows, pl.ds(at, LANES)], turn, 1))
+                for j in range(tiles):
+                    term = factor * jnp.where(mask, turned[j], turned[j + 1])
+                    total[j] = term if total[j] is None else total[j] + term
             for j in range(tiles):
                 sums[rows, j * LANES : (j + 1) * LANES] = total[j]
-            return 0
-
-        lax.fori_loop(0, ROWS // 8, shift_rows, 0)
         here = sums[:ROWS, :]
         sums[ROWS:, :] = pltpu.roll(here, width - 1, 1)
         high, low = halves(sums[...])
@@ -126,6 +178,7 @@
             y = y[: 2 * ROWS] + y[2 * ROWS :]
             cw = share[t : t + 1, n : n + step]
             proj[t * ROWS : (t + 1) * ROWS, n : n + step] = (1.0 - cw) * y[:ROWS] + cw * y[ROWS:]
+    get_col.wait()
     high, low = halves(proj[...])
     band[...] = dot(high, col_tab[0]) + dot(low, col_tab[0]) + dot(high, col_tab[1])
     for t in range(TILTS):
@@ -134,6 +187,7 @@
         last = band[b + BAND : b + BAND + 1, :]
         band[b + HALF : b + HALF + 1, :BAND] = row[:, :BAND] + last[:, BAND:]
         band[b + HALF : b + HALF + 1, BAND:] = row[:, BAND:] - last[:, :BAND]
+    get_ref.wait()
     for k in range(INNER):
         for t in range(TILTS):
             for i, (r0, c0) in enumerate(((0, 0), (0, BAND), (HALF, 0), (HALF, BAND))):
@@ -151,32 +205,30 @@
                 out[k, to : to + 1, :] = ref[0, i, a : a + 1, :]
 
 
-def row_sum_kernel(info, got, out):
+def row_sum_kernel(aux, got, out):
     n = got.shape[0]
-    mine = info[0]
     total = got[0, : 8 * PAIRS, :]
     for s in range(1, n):
         total = total + got[s, : 8 * PAIRS, :]
     refs = []
     for t in range(TILTS):
-        owner = info[1 + t]
-        piece = got[lax.rem(owner, n), 8 * PAIRS :, :]
-        refs.append(jnp.where(lax.div(owner, n) == mine, piece, 0.0))
+        at = t * (4 * PAIRS + INNER) + 4 * PAIRS
+        chosen = jnp.zeros((4 * PAIRS, BAND), jnp.float32)
+        for s in range(n):
+            chosen = jnp.where(aux[at + s : at + s + 1, :] > 0.5, got[s, 8 * PAIRS :, :], chosen)
+        refs.append(chosen)
     for y in range(out.shape[0]):
         out[y, : 8 * PAIRS, :] = total
         for t in range(TILTS):
             out[y, (8 + 4 * t) * PAIRS : (12 + 4 * t) * PAIRS, :] = refs[t]
 
 
-def cross_kernel(length, info, center, got, tab, out, lhs):
+def cross_kernel(aux, got, tab, out, lhs):
     n = got.shape[0]
     total = got[0]
     for s in range(1, n):
         total = total + got[s]
-    k = info[0]
-    b = lax.broadcasted_iota(jnp.int32, (PAIRS, BAND), 1)
-    p = k * PAIRS + lax.broadcasted_iota(jnp.int32, (PAIRS, BAND), 0)
-    zero = p == 0
+    zero = lax.axis_index("seat") * PAIRS + lax.broadcasted_iota(jnp.int32, (PAIRS, BAND), 0) == 0
     lhs[...] = jnp.zeros(lhs.shape, jnp.float32)
     energies = []
     for t in range(TILTS):
@@ -190,14 +242,15 @@
         minus = (jnp.where(zero, sc, cc + ss), -jnp.where(zero, ss, cs - sc))
         crossed = []
         e_spec = e_ref = 0.0
-        for (sr, si), (rr, ri), q in ((plus, refs[:2], p), (minus, refs[2:], jnp.where(zero, -HALF, -p))):
+        for i, ((sr, si), (rr, ri)) in enumerate(((plus, refs[:2]), (minus, refs[2:]))):
             cr = sr * rr + si * ri
             ci = si * rr - sr * ri
             e_spec = e_spec + sr * sr + si * si
             e_ref = e_ref + rr * rr + ri * ri
-            angle = ((q * center[t, 0] + b * center[t, 1]) & (length - 1)).astype(jnp.float32) * (2.0 * np.pi / length)
-            co, si_ = jnp.cos(angle), jnp.sin(angle)
-            crossed.append((cr * co - ci * si_, cr * si_ + ci * co))
+            at = t * (4 * PAIRS + INNER) + i * PAIRS
+            co = aux[at : at + PAIRS, :]
+            sn = aux[at + 2 * PAIRS : at + 3 * PAIRS, :]
+            crossed.append((cr * co - ci * sn, cr * sn + ci * co))
         (pr, pi), (mr, mi) = crossed
         at = 2 * PAIRS * t
         lhs[at : at + PAIRS, :BAND] = jnp.where(zero, pr, pr + mr)
@@ -218,18 +271,19 @@
             out[d, to : to + 1, :] = e
 
 
-def window_kernel(info, got, tab, rows, peaks, corr):
+def window_kernel(got, tab, rows, peaks, corr):
     x = got[...].reshape(got.shape[0] * CH_OUT, WIN)
     high, low = halves(x)
     c = dot(tab[0], high) + dot(tab[0], low) + dot(tab[1], high)
     e = jnp.sum(jnp.sum(got[:, 4 * PAIRS + TILTS :, :], 0), 1, keepdims=True)
+    mine_row = lax.axis_index("line") * INNER + lax.axis_index("seat")
     for t in range(TILTS):
         spec = e[2 * t : 2 * t + 1] / (BAND * BAND) + 1e-06
         ref = e[2 * t + 1 : 2 * t + 2] / (BAND * BAND) + 1e-06
         mine = c[t * WIN : (t + 1) * WIN] / (BAND * jnp.sqrt(spec * ref))
         corr[t] = mine
         peaks[t] = jnp.max(mine)
-        rows[t] = corr[t, pl.ds(info[0], 1), :]
+        rows[t] = corr[t, pl.ds(mine_row, 1), :]
 
 
 def solution(mesh):
@@ -240,59 +294,74 @@
     slab = ("line", "seat")
     vmem = pl.BlockSpec(memory_space=pltpu.VMEM)
     smem = pl.BlockSpec(memory_space=pltpu.SMEM)
-    big = pltpu.CompilerParams(vmem_limit_bytes=48 * 1024 * 1024)
+    hbm = pl.BlockSpec(memory_space=pltpu.HBM)
+    small = pltpu.CompilerParams(vmem_limit_bytes=4 * 1024 * 1024)
+    f32, bf16 = jnp.float32, jnp.bfloat16
 
     def per_device(volume, shift, weight, left, share, center, owner, ref):
         planes, height, width = volume.shape
-        line = lax.axis_index("line")
-        seat = lax.axis_index("seat")
-        f32 = jnp.float32
-        packed = pl.pallas_call(
+        row_tab = jnp.asarray(row_table(height))
+        col_tab = jnp.asarray(column_table(width))
+        blocks = planes * width // 256
+        packed, aux = pl.pallas_call(
             spectrum_kernel,
-            out_shape=jax.ShapeDtypeStruct((INNER, CH_IN, BAND), f32),
-            in_specs=[smem, smem] + [vmem] * 6,
-            out_specs=vmem,
+            out_shape=[
+                jax.ShapeDtypeStruct((INNER, CH_IN, BAND), f32),
+                jax.ShapeDtypeStruct((TILTS * (4 * PAIRS + INNER), BAND), f32),
+            ],
+            in_specs=[hbm] * 10,
+            out_specs=[vmem] * 2,
             scratch_shapes=[
+                pltpu.SMEM(shift.shape, jnp.int32),
+                pltpu.SMEM(weight.shape, f32),
+                pltpu.SMEM(center.shape, jnp.int32),
+                pltpu.SMEM(owner.shape, jnp.int32),
+                pltpu.VMEM((blocks, height, 256), bf16),
+                pltpu.VMEM(row_tab.shape, bf16),
+                pltpu.VMEM(col_tab.shape, bf16),
+                pltpu.VMEM(left.shape, jnp.int32),
+                pltpu.VMEM(share.shape, f32),
+                pltpu.VMEM(ref.shape, f32),
                 pltpu.VMEM((planes, ROWS, width + 2 * LANES), f32),
                 pltpu.VMEM((2 * ROWS, width), f32),
-                pltpu.VMEM((4 * ROWS, width), jnp.bfloat16),
+                pltpu.VMEM((4 * ROWS, width), bf16),
                 pltpu.VMEM((TILTS * ROWS, width), f32),
                 pltpu.VMEM((TILTS * ROWS, 2 * BAND), f32),
+                pltpu.SemaphoreType.DMA((9,)),
+                pltpu.SemaphoreType.DMA((blocks,)),
             ],
-            compiler_params=big,
+            compiler_params=pltpu.CompilerParams(vmem_limit_bytes=32 * 1024 * 1024),
             name="spectrum",
-        )(shift, weight, volume, jnp.asarray(row_table(height)), jnp.asarray(column_table(width)), left, share, ref)
+        )(*(pltpu.with_memory_space_constraint(a, pltpu.HBM) for a in (shift, weight, center, owner, volume, row_tab, col_tab, left, share, ref)))
         got = lax.all_to_all(packed, "seat", 0, 0, tiled=True)
-        info = jnp.concatenate([line[None], owner[:TILTS]]).astype(jnp.int32)
         summed = pl.pallas_call(
             row_sum_kernel,
             out_shape=jax.ShapeDtypeStruct((outer, CH_MID, BAND), f32),
-            in_specs=[smem, vmem],
+            in_specs=[vmem] * 2,
             out_specs=vmem,
+            compiler_params=small,
             name="row_sum",
-        )(info, got)
+        )(aux, got)
         got = lax.all_to_all(summed, "line", 0, 0, tiled=True)
-
-        def cross(*refs):
-            cross_kernel(width, *refs)
-
         piece = pl.pallas_call(
-            cross,
+            cross_kernel,
             out_shape=jax.ShapeDtypeStruct((INNER, CH_OUT, WIN), f32),
-            in_specs=[smem, smem, vmem, vmem],
+            in_specs=[vmem] * 3,
             out_specs=vmem,
             scratch_shapes=[pltpu.VMEM((32, 2 * BAND), f32)],
+            compiler_params=small,
             name="cross",
-        )(seat[None].astype(jnp.int32), center, got, jnp.asarray(window_column_table(width)))
+        )(aux, got, jnp.asarray(window_column_table(width)))
         got = lax.all_to_all(piece, "seat", 0, 0, tiled=True)
         rows, peaks = pl.pallas_call(
             window_kernel,
             out_shape=[jax.ShapeDtypeStruct((TILTS, 1, WIN), f32), jax.ShapeDtypeStruct((TILTS,), f32)],
-            in_specs=[smem, vmem, vmem],
+            in_specs=[vmem] * 2,
             out_specs=[vmem, smem],
             scratch_shapes=[pltpu.VMEM((TILTS, WIN, WIN), f32)],
+            compiler_params=small,
             name="window",
-        )((line * INNER + seat)[None].astype(jnp.int32), got, jnp.asarray(window_row_table(height)))
+        )(got, jnp.asarray(window_row_table(height)))
         return rows, peaks
 
     placed = (

time: 95.9 us -> 77 us (0.80)
  blocking collectives: 0 us -> 65.2 us
  waiting for transfers between devices: 36.3 us -> 0 us
  starting transfers between devices: 31.1 us -> 0 us
  local copies, waits for them, and re-layouts: 8.06 us -> 0.01 us
  Pallas kernels: 18.6 us -> 10.9 us
    all_to_all x0 -> x3, blocking collectives: none -> 65.2 us  [the longest x1 37.6 us: per_device(): got = lax.all_to_all(packed, 'seat', 0, 0, tiled=True)]
    all_to_all x3 -> x0, waiting for transfers between devices: 36.3 us -> none  [the longest x1 14.1 us: per_device(): got = lax.all_to_all(packed, 'seat', 0, 0, tiled=True)]
    all_to_all x3 -> x0, starting transfers between devices: 31.1 us -> none  [the longest x1 23.8 us: per_device(): got = lax.all_to_all(packed, 'seat', 0, 0, tiled=True)]
    unnamed x22 -> x4, local copies, waits for them, and re-layouts: 8.06 us -> 0.01 us
    pallas_call x2, Pallas kernels: 14.7 us -> 9.78 us  [the longest x1 9.57 us: per_device(): pl.pallas_call(spectrum_kernel, out_shape=[jax.ShapeDtypeStruct((INNER, C...]
    pallas_call x1, Pallas kernels: 1.74 us -> 0.05 us  [per_device(): pl.pallas_call(row_sum_kernel, out_shape=jax.ShapeDtypeStruct((outer, CH_...]
    pallas_call x1, Pallas kernels: 2.16 us -> 1.06 us  [per_device(): pl.pallas_call(window_kernel, out_shape=[jax.ShapeDtypeStruct((TILTS, 1,...]
  transfers between devices with their start and end apart: 3 -> 0, of which waited for: 3 -> 0; matrix products, arithmetic and copies ran while one was open for 1% -> 0% of each run, Pallas kernels for 0% -> 0%
where the time goes in v2:
time: 77 us; the launch traced here: 76.8 us
  blocking collectives  65.2 us (85%)
  Pallas kernels  10.9 us (14%)
    all_to_all x1, blocking collectives, per_device(): got = lax.all_to_all(packed, 'seat', 0, 0, tiled=True)  37.6 us
    all_to_all x1, blocking collectives, per_device(): got = lax.all_to_all(summed, 'line', 0, 0, tiled=True)  14.2 us
    all_to_all x1, blocking collectives, per_device(): got = lax.all_to_all(piece, 'seat', 0, 0, tiled=True)  13.4 us
    pallas_call x1, Pallas kernels, per_device(): pl.pallas_call(spectrum_kernel, out_shape=[jax.ShapeDtypeStruct((INNER, C...  9.57 us

profile of v2, /device:TPU:513, one launch (start us, length us, event | category | flops | bytes accessed | tf_op | source)
XLA Modules:
  0.0 76.8 jit_solution(17421364583380095334)
XLA Ops:
  0.6 0.0 copy-start.1
  0.6 0.0 copy-start
  0.7 9.6 %spectrum.1 = (f32[16,48,128]{2,1,0:T(8,128)S(1)}, f32[64,128]{1,0:T(8,128)S(1)}) custom-call(s32[2,2]{1,0:T(2,128)} %h_shift.1, f32[2,2]{1,0:T(2,128)} %h_weight.1, s32[2,2]{1,0:T(2,128)} %h_center.1, s32[128]{0:T(128)} %h_owner.1, bf16[2,1024,1024]{2,1,0:T(8,128)(2,1)} %h_volume.1, bf16[272,1024]{1,0:T(8,128)(2,1)} %constant.8.clone.h_row, ...), custom_call_target="tpu_custom_call" | custom-call | tf_op jit(solution)/shard_map/spectrum/pallas_call | solution.py:306
  10.2 37.6 %all_to_all.15.got = f32[16,48,128]{2,1,0:T(8,128)S(1)} all-to-all(f32[16,48,128]{2,1,0:T(8,128)S(1)} %get-tuple-element.5), channel_id=1, replica_groups=mesh['grp'=2,'line'=8,'seat'=16] {'seat'}, dimensions={0} | all-to-all | bytes 786432 | tf_op jit(solution)/shard_map/all_to_all | solution.py:336
  47.8 14.2 %all_to_all.16.got = f32[8,64,128]{2,1,0:T(8,128)S(1)} all-to-all(f32[8,64,128]{2,1,0:T(8,128)S(1)} %row_sum.1), channel_id=1, replica_groups=mesh['grp'=2,'line'=8,'seat'=16] {'line'}, dimensions={0} | all-to-all | bytes 524288 | tf_op jit(solution)/shard_map/all_to_all | solution.py:345
  62.1 0.0 copy-done.1
  62.1 0.2 cross.1
  62.3 13.4 %all_to_all.17.got = f32[16,24,128]{2,1,0:T(8,128)S(1)} all-to-all(f32[16,24,128]{2,1,0:T(8,128)S(1)} %cross.1), channel_id=1, replica_groups=mesh['grp'=2,'line'=8,'seat'=16] {'seat'}, dimensions={0} | all-to-all | bytes 393216 | tf_op jit(solution)/shard_map/all_to_all | solution.py:355
  75.7 0.0 copy-done
  75.7 1.1 %window.1 = (f32[2,1,128]{2,1,0:T(1,128)}, f32[2]{0:T(128)}) custom-call(f32[16,24,128]{2,1,0:T(8,128)S(1)} %all_to_all.17.got, bf16[2,256,384]{2,1,0:T(8,128)(2,1)S(1)} %copy-done), custom_call_target="tpu_custom_call" | custom-call | tf_op jit(solution)/shard_map/window/pallas_call | solution.py:356
  (1 shorter events, 0.0 us)
Async XLA Ops:
  0.6 61.4 %copy-start.1 = (bf16[2,256,128]{2,1,0:T(8,128)(2,1)S(1)}, bf16[2,256,128]{2,1,0:T(8,128)(2,1)}, u32[]{:S(2)}) copy-start(bf16[2,256,128]{2,1,0:T(8,128)(2,1)} %constant.10.clone.tab) | copy-start | bytes 393220
  0.6 75.1 %copy-start = (bf16[2,256,384]{2,1,0:T(8,128)(2,1)S(1)}, bf16[2,256,384]{2,1,0:T(8,128)(2,1)}, u32[]{:S(2)}) copy-start(bf16[2,256,384]{2,1,0:T(8,128)(2,1)} %constant.11.clone.tab) | copy-start | bytes 1179652

commit v3 on v2

v3 whole, which is shorter than its diff:
```python
import numpy as np

import jax
import jax.numpy as jnp
from jax import lax
from jax.experimental import pallas as pl
from jax.experimental.pallas import tpu as pltpu
from jax.sharding import Mesh, PartitionSpec as P
import ml_dtypes

BAND = 128
HALF = BAND // 2
WIN = 128
TILTS = 2
CORES = 2
COLS = 8
ROWS = 136
LANES = 128
CHUNK = 8
CH_OUT = 4


def split(table):
    table = np.asarray(table, np.float32)
    high = table.astype(ml_dtypes.bfloat16)
    low = (table - high.astype(np.float32)).astype(ml_dtypes.bfloat16)
    return high, low


def turns(a, b, length):
    angle = (a[:, None].astype(np.int64) * b[None, :]) % length * (2.0 * np.pi / length)
    return np.cos(angle), np.sin(angle)


def row_table(length):
    c, s = turns(np.arange(HALF + 1), np.arange(length), length)
    out = np.zeros((ROWS, length))
    out[:HALF] = c[:HALF]
    out[HALF] = c[HALF]
    out[HALF + 1 : BAND] = s[1:HALF]
    out[BAND] = s[HALF]
    high, low = split(out)
    return np.concatenate([high, low])


def column_table(length):
    c, s = turns(np.arange(length), np.arange(BAND), length)
    high, low = split(np.concatenate([c, s], 1))
    return np.stack([high, low])


def window_column_table(length):
    c, s = turns(np.arange(BAND), np.arange(WIN) - WIN // 2, length)
    high, low = split(np.concatenate([c, -s], 0))
    return np.stack([high, low])


def window_row_table(length):
    c, s = turns(np.arange(WIN) - WIN // 2, np.arange(HALF + 1), length)
    out = np.zeros((WIN, HALF, CH_OUT))
    out[:, :, 0] = c[:, :HALF]
    out[:, 1:, 1] = -s[:, 1:HALF]
    out[:, 0, 1] = c[:, HALF]
    out[:, 0, 2] = s[:, HALF]
    high, low = split(out.reshape(WIN, HALF * CH_OUT))
    return np.stack([high, low])


def dot(a, b):
    return jnp.dot(a, b, preferred_element_type=jnp.float32)


def halves(x):
    high = x.astype(jnp.bfloat16)
    return high, (x - high.astype(jnp.float32)).astype(jnp.bfloat16)


def shift_kernel(
    h_shift, h_weight, h_center, h_owner, h_volume, h_row, h_ref, keep, send, aux,
    shift, weight, center, owner, volume, row_tab, rpad, sem, vsem,
):
    planes, height, width = h_volume.shape
    tiles = width // LANES
    step = 256
    steps = height // step

    def fetch(src, dst, i):
        copy = pltpu.make_async_copy(src, dst, sem.at[i])
        copy.start()
        return copy

    get_row = fetch(h_row, row_tab, 0)
    blocks = []
    for z in range(planes):
        for n in range(steps):
            i = z * steps + n
            cut = pl.ds(n * step, step)
            copy = pltpu.make_async_copy(h_volume.at[z, cut, :], volume.at[z, cut, :], vsem.at[i])
            copy.start()
            blocks.append(copy)
            if i == 0:
                get_center = fetch(h_center, center, 1)
                get_owner = fetch(h_owner, owner, 2)
                get_shift = fetch(h_shift, shift, 3)
                get_weight = fetch(h_weight, weight, 4)
    refs = [fetch(h_ref.at[0, i], send.at[pl.ds(tiles * ROWS + i * BAND, BAND), :], 5 + i) for i in range(2)]

    col = lax.axis_index("col")
    core = lax.axis_index("core")
    rpad[:, :, :LANES] = jnp.zeros((planes, ROWS, LANES), jnp.float32)
    rpad[:, :, LANES + width :] = jnp.zeros((planes, ROWS, LANES), jnp.float32)
    get_center.wait()
    get_owner.wait()
    pair = lax.axis_index("line") * COLS + col
    row = lax.broadcasted_iota(jnp.int32, (8, BAND), 0)
    b = lax.broadcasted_iota(jnp.int32, (8, BAND), 1)
    q = jnp.where(row == 0, pair, jnp.where(pair == 0, -HALF, -pair))
    turn = (q * center[core, 0] + b * center[core, 1]) & (width - 1)
    angle = turn.astype(jnp.float32) * (2.0 * np.pi / width)
    aux[:8, :] = jnp.cos(angle)
    aux[8:16, :] = jnp.sin(angle)
    who = pair * CORES + jnp.where(row == 0, core, 1 - core)
    aux[16:, :] = jnp.where(who == owner[core], 1.0, 0.0)

    get_row.wait()
    for z in range(planes):
        for n in range(steps):
            blocks[z * steps + n].wait()
        for n in range(0, width, step):
            r = dot(row_tab[...], volume[z, :, n : n + step])
            rpad[z, :, LANES + n : LANES + n + step] = r[:ROWS] + r[ROWS:]
    get_shift.wait()
    get_weight.wait()
    lane = lax.broadcasted_iota(jnp.int32, (8, LANES), 1)
    for t, out in ((1 - core, send), (core, keep)):
        moves = []
        for z in range(planes):
            w = weight[t, z]
            for more, factor in ((0, 1.0 - w), (1, w)):
                s = shift[t, z] + more
                turn = jnp.where(s < 0, s + LANES, s)
                moves.append((z, jnp.where(s < 0, 1, 0), turn, lane < turn, factor))
        for g in range(ROWS // 8):
            rows = slice(g * 8, g * 8 + 8)
            total = [None] * tiles
            for z, off, turn, mask, factor in moves:
                turned = []
                for j in range(tiles + 1):
                    at = pl.multiple_of((j + off) * LANES, LANES)
                    turned.append(pltpu.roll(rpad[z, rows, pl.ds(at, LANES)], turn, 1))
                for j in range(tiles):
                    term = factor * jnp.where(mask, turned[j], turned[j + 1])
                    total[j] = term if total[j] is None else total[j] + term
            for j in range(tiles):
                at = j * ROWS + g * 8
                out[at : at + 8, :] = total[j]
    for copy in refs:
        copy.wait()


def band_kernel(keep, sent, came, aux, left, share, col_tab, out, sums, lhs, proj, band, own):
    width = left.shape[1]
    tiles = width // LANES
    step = 256
    core = lax.axis_index("core")
    for j in range(tiles):
        rows = slice(j * ROWS, (j + 1) * ROWS)
        sums[:ROWS, j * LANES : (j + 1) * LANES] = keep[rows, :] + came[rows, :]
    sums[ROWS:, :] = pltpu.roll(sums[:ROWS, :], width - 1, 1)
    high, low = halves(sums[...])
    lhs[: 2 * ROWS] = high
    lhs[2 * ROWS :] = low
    place = lax.broadcasted_iota(jnp.int32, (width, step), 0)
    for n in range(0, width, step):
        pick = jnp.where(place == left[pl.ds(core, 1), n : n + step], 1.0, 0.0).astype(jnp.bfloat16)
        y = dot(lhs[...], pick)
        y = y[: 2 * ROWS] + y[2 * ROWS :]
        cw = share[pl.ds(core, 1), n : n + step]
        proj[:, n : n + step] = (1.0 - cw) * y[:ROWS] + cw * y[ROWS:]
    high, low = halves(proj[...])
    band[...] = dot(high, col_tab[0]) + dot(low, col_tab[0]) + dot(high, col_tab[1])
    row = band[HALF : HALF + 1, :]
    last = band[BAND : BAND + 1, :]
    band[HALF : HALF + 1, :BAND] = row[:, :BAND] + last[:, BAND:]
    band[HALF : HALF + 1, BAND:] = row[:, BAND:] - last[:, :BAND]
    mine = aux[16:17, :] > 0.5
    theirs = aux[17:18, :] > 0.5
    for i in range(2):
        at = slice(tiles * ROWS + i * BAND, tiles * ROWS + (i + 1) * BAND)
        own[i] = jnp.where(mine, sent[at, :], jnp.where(theirs, came[at, :], 0.0))
    for p in range(HALF):
        minus = HALF - p if p else 0
        for i in range(2):
            out[p, i : i + 1, :] = band[p : p + 1, i * BAND : (i + 1) * BAND]
            out[p, 2 + i : 3 + i, :] = band[HALF + p : HALF + p + 1, i * BAND : (i + 1) * BAND]
            out[p, 4 + i : 5 + i, :] = own[i, HALF + p : HALF + p + 1, :]
            out[p, 6 + i : 7 + i, :] = own[i, minus : minus + 1, :]


def cross_kernel(aux, got, tab, out, lhs):
    n = got.shape[0]
    parts = [got[i] for i in range(8)]
    for i in range(8, n):
        parts[i % 8] = parts[i % 8] + got[i]
    while len(parts) > 1:
        parts = [parts[i] + parts[i + 1] for i in range(0, len(parts), 2)]
    total = parts[0]
    pair = lax.axis_index("line") * COLS + lax.axis_index("col")
    zero = lax.broadcasted_iota(jnp.int32, (1, BAND), 1) * 0 + pair == 0
    cc, cs, sc, ss, *refs = (total[i : i + 1, :] for i in range(8))
    plus = (jnp.where(zero, cc, cc - ss), -jnp.where(zero, cs, cs + sc))
    minus = (jnp.where(zero, sc, cc + ss), -jnp.where(zero, ss, cs - sc))
    crossed = []
    e_spec = e_ref = 0.0
    for i, ((sr, si), (rr, ri)) in enumerate(((plus, refs[:2]), (minus, refs[2:]))):
        cr = sr * rr + si * ri
        ci = si * rr - sr * ri
        e_spec = e_spec + sr * sr + si * si
        e_ref = e_ref + rr * rr + ri * ri
        co = aux[i : i + 1, :]
        sn = aux[8 + i : 9 + i, :]
        crossed.append((cr * co - ci * sn, cr * sn + ci * co))
    (pr, pi), (mr, mi) = crossed
    lhs[...] = jnp.zeros(lhs.shape, jnp.float32)
    lhs[0:1, :BAND] = jnp.where(zero, pr, pr + mr)
    lhs[0:1, BAND:] = jnp.where(zero, pi, pi + mi)
    lhs[1:2, :BAND] = jnp.where(zero, mr, pi - mi)
    lhs[1:2, BAND:] = jnp.where(zero, mi, mr - pr)
    lhs[2:3, :BAND] = mi
    lhs[2:3, BAND:] = -mr
    high, low = halves(lhs[...])
    h = dot(high, tab[0]) + dot(low, tab[0]) + dot(high, tab[1])
    lane = lax.broadcasted_iota(jnp.int32, (1, BAND), 1)
    e_spec = jnp.sum(e_spec, 1, keepdims=True)
    e_ref = jnp.sum(e_ref, 1, keepdims=True)
    lhs[:8, :BAND] = h[:8]
    lhs[3:4, :BAND] = jnp.where(lane < BAND // 2, e_spec, e_ref)
    done = lhs[:CH_OUT, :BAND]
    for d in range(out.shape[0]):
        out[d] = done


def window_kernel(got, tab, send, keep):
    n = got.shape[0]
    mine_row = (lax.axis_index("line") * COLS + lax.axis_index("col")) * CORES + lax.axis_index("core")
    high, low = halves(got[...].reshape(n * CH_OUT, WIN))
    c = dot(tab[0], high) + dot(tab[0], low) + dot(tab[1], high)
    e = jnp.sum(got[:, CH_OUT - 1, :], 0, keepdims=True)
    spec = e[:, :1] / (BAND * BAND) + 1e-06
    ref = e[:, BAND - 1 :] / (BAND * BAND) + 1e-06
    c = c / (BAND * jnp.sqrt(spec * ref))
    peak = jnp.max(c)
    index = lax.broadcasted_iota(jnp.int32, (WIN, WIN), 0)
    for out, row in ((keep, mine_row), (send, mine_row ^ 1)):
        out[0:1, :] = jnp.sum(jnp.where(index == row, c, 0.0), 0, keepdims=True)
        out[1:2, :] = jnp.full((1, WIN), peak)


def join_kernel(keep, came, rows, peaks):
    core = lax.axis_index("core")
    rows[pl.ds(core, 1), 0, :] = keep[0:1, :]
    rows[pl.ds(1 - core, 1), 0, :] = came[0:1, :]
    peaks[core] = jnp.max(keep[1:2, :])
    peaks[1 - core] = jnp.max(came[1:2, :])


def solution(mesh):
    lines = mesh.shape["slab"] // (COLS * CORES)
    grid = Mesh(
        mesh.devices.reshape(mesh.shape["grp"], lines, COLS, CORES), ("grp", "line", "col", "core")
    )
    slab = ("line", "col", "core")
    vmem = pl.BlockSpec(memory_space=pltpu.VMEM)
    smem = pl.BlockSpec(memory_space=pltpu.SMEM)
    hbm = pl.BlockSpec(memory_space=pltpu.HBM)
    small = pltpu.CompilerParams(vmem_limit_bytes=4 * 1024 * 1024)
    f32, bf16 = jnp.float32, jnp.bfloat16

    def per_device(volume, shift, weight, left, share, center, owner, ref):
        planes, height, width = volume.shape
        row_tab = jnp.asarray(row_table(height))
        col_tab = jnp.asarray(column_table(width))
        tiles = width // LANES
        blocks = planes * height // 256
        fetched = (shift, weight, center, owner, volume, row_tab, ref)
        keep, send, aux = pl.pallas_call(
            shift_kernel,
            out_shape=[
                jax.ShapeDtypeStruct((tiles * ROWS, LANES), f32),
                jax.ShapeDtypeStruct((tiles * ROWS + 2 * BAND, LANES), f32),
                jax.ShapeDtypeStruct((24, BAND), f32),
            ],
            in_specs=[hbm] * len(fetched),
            out_specs=[vmem] * 3,
            scratch_shapes=[
                pltpu.SMEM(shift.shape, jnp.int32),
                pltpu.SMEM(weight.shape, f32),
                pltpu.SMEM(center.shape, jnp.int32),
                pltpu.SMEM(owner.shape, jnp.int32),
                pltpu.VMEM(volume.shape, bf16),
                pltpu.VMEM(row_tab.shape, bf16),
                pltpu.VMEM((planes, ROWS, width + 2 * LANES), f32),
                pltpu.SemaphoreType.DMA((7,)),
                pltpu.SemaphoreType.DMA((blocks,)),
            ],
            compiler_params=pltpu.CompilerParams(vmem_limit_bytes=24 * 1024 * 1024),
            name="shift",
        )(*(pltpu.with_memory_space_constraint(a, pltpu.HBM) for a in fetched))
        came = lax.ppermute(send, "core", [(i, (i + 1) % CORES) for i in range(CORES)])
        packed = pl.pallas_call(
            band_kernel,
            out_shape=jax.ShapeDtypeStruct((HALF, CHUNK, BAND), f32),
            in_specs=[vmem] * 7,
            out_specs=vmem,
            scratch_shapes=[
                pltpu.VMEM((2 * ROWS, width), f32),
                pltpu.VMEM((4 * ROWS, width), bf16),
                pltpu.VMEM((ROWS, width), f32),
                pltpu.VMEM((ROWS, 2 * BAND), f32),
                pltpu.VMEM((2, BAND, BAND), f32),
            ],
            compiler_params=pltpu.CompilerParams(vmem_limit_bytes=24 * 1024 * 1024),
            name="band",
        )(keep, send, came, aux, left, share, col_tab)
        got = lax.all_to_all(packed, ("line", "col"), 0, 0, tiled=True)
        piece = pl.pallas_call(
            cross_kernel,
            out_shape=jax.ShapeDtypeStruct((HALF, CH_OUT, WIN), f32),
            in_specs=[vmem] * 3,
            out_specs=vmem,
            scratch_shapes=[pltpu.VMEM((16, 2 * BAND), f32)],
            compiler_params=small,
            name="cross",
        )(aux, got, jnp.asarray(window_column_table(width)))
        got = lax.all_to_all(piece, ("line", "col"), 0, 0, tiled=True)
        send, keep = pl.pallas_call(
            window_kernel,
            out_shape=[jax.ShapeDtypeStruct((2, WIN), f32)] * 2,
            in_specs=[vmem] * 2,
            out_specs=[vmem] * 2,
            compiler_params=small,
            name="window",
        )(got, jnp.asarray(window_row_table(height)))
        came = lax.ppermute(send, "core", [(i, (i + 1) % CORES) for i in range(CORES)])
        return pl.pallas_call(
            join_kernel,
            out_shape=[jax.ShapeDtypeStruct((TILTS, 1, WIN), f32), jax.ShapeDtypeStruct((TILTS,), f32)],
            in_specs=[vmem] * 2,
            out_specs=[vmem, smem],
            compiler_params=small,
            name="join",
        )(keep, came)

    placed = (
        P(("grp",) + slab, None, None),
        P("grp", slab),
        P("grp", slab),
        P("grp", None),
        P("grp", None),
        P("grp", None),
        P("grp"),
        P(("grp",) + slab, None, None, None),
    )
    return jax.shard_map(
        per_device,
        mesh=grid,
        in_specs=placed,
        out_specs=(P("grp", slab, None), P("grp")),
        check_vma=False,
    )
```

time: 77 us -> 69.6 us (0.904)
  blocking collectives: 65.2 us -> 34.6 us
  starting transfers between devices: 0 us -> 23.3 us
  Pallas kernels: 10.9 us -> 8.19 us
  waiting for transfers between devices: 0 us -> 2.59 us
    all_to_all x3 -> x2, blocking collectives: 65.2 us -> 34.6 us  [the longest x1 17.7 us: per_device(): got = lax.all_to_all(packed, ('line', 'col'), 0, 0, tiled=True)]
    ppermute x0 -> x2, starting transfers between devices: none -> 23.3 us  [per_device(): lax.ppermute(send, 'core', [(i, (i + 1) % CORES) for i in range(CORES)])]
    pallas_call x4 -> x5, Pallas kernels: 10.9 us -> 8.19 us  [the longest x1 4.81 us: per_device(): pl.pallas_call(shift_kernel, out_shape=[jax.ShapeDtypeStruct((tiles * ROW...]
    ppermute x0 -> x2, waiting for transfers between devices: none -> 2.59 us  [per_device(): lax.ppermute(send, 'core', [(i, (i + 1) % CORES) for i in range(CORES)])]
  transfers between devices with their start and end apart: 0 -> 2, of which waited for: 0 -> 2; matrix products, arithmetic and copies ran while one was open for 0% -> 0% of each run, Pallas kernels for 0% -> 0%
where the time goes in v3:
time: 69.6 us; the launch traced here: 69.5 us
  blocking collectives  34.6 us (50%)
  starting transfers between devices  23.3 us (33%)
  Pallas kernels  8.19 us (12%)
  waiting for transfers between devices  2.59 us (4%)
  between operations  0.71 us (1%)
    ppermute x2, starting transfers between devices, per_device(): lax.ppermute(send, 'core', [(i, (i + 1) % CORES) for i in range(CORES)])  23.3 us
    all_to_all x1, blocking collectives, per_device(): got = lax.all_to_all(packed, ('line', 'col'), 0, 0, tiled=True)  17.7 us
    all_to_all x1, blocking collectives, per_device(): got = lax.all_to_all(piece, ('line', 'col'), 0, 0, tiled=True)  16.9 us
    pallas_call x1, Pallas kernels, per_device(): pl.pallas_call(shift_kernel, out_shape=[jax.ShapeDtypeStruct((tiles * ROW...  4.81 us
    ppermute x2, waiting for transfers between devices, per_device(): lax.ppermute(send, 'core', [(i, (i + 1) % CORES) for i in range(CORES)])  2.59 us
    pallas_call x1, Pallas kernels, per_device(): pl.pallas_call(band_kernel, out_shape=jax.ShapeDtypeStruct((HALF, CHUNK,...  2.21 us
  transfers between devices with their start and end apart: 2, of which 2 were waited for; matrix products, arithmetic and copies ran while one was open for 0% of the time, Pallas kernels for 0%

profile of v3, /device:TPU:513, one launch (start us, length us, event | category | flops | bytes accessed | tf_op | source)
XLA Modules:
  0.0 69.5 jit_solution(12616429021811651977)
XLA Ops:
  0.6 0.0 copy-start
  0.6 0.0 copy-start.2
  0.7 0.0 copy-start.1
  0.7 0.0 copy-start.4
  0.7 0.0 copy-start.3
  0.7 4.8 %shift.1 = (f32[1088,128]{1,0:T(8,128)S(1)}, f32[1344,128]{1,0:T(8,128)S(1)}, f32[24,128]{1,0:T(8,128)S(1)}) custom-call(s32[2,2]{1,0:T(2,128)} %h_shift.1, f32[2,2]{1,0:T(2,128)} %h_weight.1, s32[2,2]{1,0:T(2,128)} %h_center.1, s32[128]{0:T(128)} %h_owner.1, bf16[2,1024,1024]{2,1,0:T(8,128)(2,1)} %h_volume.1, bf16[272,1024]{1,0:T(8,128)(2,1)} %constant.8.clone.h_row, ...), custom_call_target="tpu_custom_call" | custom-call | tf_op jit(solution)/shard_map/shift/pallas_call | solution.py:286
  5.5 20.5 %collective-permute-start = (f32[1344,128]{1,0:T(8,128)S(1)}, f32[1344,128]{1,0:T(8,128)S(1)}, u32[]{:S(2)}, u32[]{:S(2)}) collective-permute-start(f32[1344,128]{1,0:T(8,128)S(1)} %get-tuple-element.9.sent), channel_id=1, source_target_pairs={{0,1},{1,0},{2,3},{3,2},{4,5},{5,4},{6,7},{7,6},{8,9},{9,8},{10,11... | collective-permute-start | bytes 2064392 | tf_op jit(solution)/shard_map/ppermute | solution.py:309
  26.1 1.8 %collective-permute-done.came = f32[1344,128]{1,0:T(8,128)S(1)} collective-permute-done((f32[1344,128]{1,0:T(8,128)S(1)}, f32[1344,128]{1,0:T(8,128)S(1)}, u32[]{:S(2)}, u32[]{:S(2)}) %collective-permute-start) | collective-permute-done | bytes 688160 | tf_op jit(solution)/shard_map/ppermute | solution.py:309
  27.8 0.0 copy-done
  27.8 0.0 copy-done.4
  27.8 0.0 copy-done.3
  27.8 2.2 %band.1 = f32[64,8,128]{2,1,0:T(8,128)S(1)} custom-call(f32[1088,128]{1,0:T(8,128)S(1)} %get-tuple-element.8.keep, f32[1344,128]{1,0:T(8,128)S(1)} %get-tuple-element.9.sent, f32[1344,128]{1,0:T(8,128)S(1)} %collective-permute-done.came, f32[24,128]{1,0:T(8,128)S(1)} %get-tuple-element.7.aux, s32[2,1024]{1,0:T(2,128)S(1)} %copy-done.3, ...), custom_call_target="tpu_custom_call" | custom-call | tf_op jit(solution)/shard_map/band/pallas_call | solution.py:310
  30.0 17.7 %all_to_all.10.got = f32[64,8,128]{2,1,0:T(8,128)S(1)} all-to-all(f32[64,8,128]{2,1,0:T(8,128)S(1)} %band.1), channel_id=1, replica_groups=mesh['grp'=2,'line'=8,'col'=8,'core'=2] {'line','col'}, dimensions={0} | all-to-all | bytes 524288 | tf_op jit(solution)/shard_map/all_to_all | solution.py:325
  47.7 0.0 copy-done.2
  47.7 0.2 cross.1
  47.9 16.9 %all_to_all.11.got = f32[64,4,128]{2,1,0:T(4,128)S(1)} all-to-all(f32[64,4,128]{2,1,0:T(4,128)S(1)} %cross.1), channel_id=1, replica_groups=mesh['grp'=2,'line'=8,'col'=8,'core'=2] {'line','col'}, dimensions={0} | all-to-all | bytes 262144 | tf_op jit(solution)/shard_map/all_to_all | solution.py:335
  64.9 0.0 copy-done.1
  64.9 0.3 window.1
  65.2 2.8 %collective-permute-start.1 = (f32[2,128]{1,0:T(2,128)S(1)}, f32[2,128]{1,0:T(2,128)S(1)}, u32[]{:S(2)}, u32[]{:S(2)}) collective-permute-start(f32[2,128]{1,0:T(2,128)S(1)} %get-tuple-element.11), channel_id=1, source_target_pairs={{0,1},{1,0},{2,3},{3,2},{4,5},{5,4},{6,7},{7,6},{8,9},{9,8},{10,11... | collective-permute-start | bytes 3080 | tf_op jit(solution)/shard_map/ppermute | solution.py:344
  68.0 0.8 %collective-permute-done.1.came = f32[2,128]{1,0:T(2,128)S(1)} collective-permute-done((f32[2,128]{1,0:T(2,128)S(1)}, f32[2,128]{1,0:T(2,128)S(1)}, u32[]{:S(2)}, u32[]{:S(2)}) %collective-permute-start.1) | collective-permute-done | bytes 1056 | tf_op jit(solution)/shard_map/ppermute | solution.py:344
  68.8 0.6 join.1
Async XLA Ops:
  0.6 27.2 %copy-start = (bf16[2,1024,256]{2,1,0:T(8,128)(2,1)S(1)}, bf16[2,1024,256]{2,1,0:T(8,128)(2,1)}, u32[]{:S(2)}) copy-start(bf16[2,1024,256]{2,1,0:T(8,128)(2,1)} %constant.9.clone.col_tab) | copy-start | bytes 3145732
  0.6 47.1 %copy-start.2 = (bf16[2,256,128]{2,1,0:T(8,128)(2,1)S(1)}, bf16[2,256,128]{2,1,0:T(8,128)(2,1)}, u32[]{:S(2)}) copy-start(bf16[2,256,128]{2,1,0:T(8,128)(2,1)} %constant.10.clone.tab) | copy-start | bytes 393220
  0.7 64.2 %copy-start.1 = (bf16[2,128,256]{2,1,0:T(8,128)(2,1)S(1)}, bf16[2,128,256]{2,1,0:T(8,128)(2,1)}, u32[]{:S(2)}) copy-start(bf16[2,128,256]{2,1,0:T(8,128)(2,1)} %constant.11.clone.tab) | copy-start | bytes 393220
  0.7 27.2 %copy-start.4 = (f32[2,1024]{1,0:T(2,128)S(1)}, f32[2,1024]{1,0:T(2,128)}, u32[]{:S(2)}) copy-start(f32[2,1024]{1,0:T(2,128)} %share.1) | copy-start | bytes 24580
  0.7 27.2 %copy-start.3 = (s32[2,1024]{1,0:T(2,128)S(1)}, s32[2,1024]{1,0:T(2,128)}, u32[]{:S(2)}) copy-start(s32[2,1024]{1,0:T(2,128)} %left.1) | copy-start | bytes 24580
  5.5 22.3 %collective-permute-start = (f32[1344,128]{1,0:T(8,128)S(1)}, f32[1344,128]{1,0:T(8,128)S(1)}, u32[]{:S(2)}, u32[]{:S(2)}) collective-permute-start(f32[1344,128]{1,0:T(8,128)S(1)} %get-tuple-element.9.sent), channel_id=1, source_target_pairs={{0,1},{1,0},{2,3},{3,2},{4,5},{5,4},{6,7},{7,6},{8,9},{9,8},{10,11... | collective-permute-start | bytes 2064392 | tf_op jit(solution)/shard_map/ppermute | solution.py:309
  65.2 3.6 %collective-permute-start.1 = (f32[2,128]{1,0:T(2,128)S(1)}, f32[2,128]{1,0:T(2,128)S(1)}, u32[]{:S(2)}, u32[]{:S(2)}) collective-permute-start(f32[2,128]{1,0:T(2,128)S(1)} %get-tuple-element.11), channel_id=1, source_target_pairs={{0,1},{1,0},{2,3},{3,2},{4,5},{5,4},{6,7},{7,6},{8,9},{9,8},{10,11... | collective-permute-start | bytes 3080 | tf_op jit(solution)/shard_map/ppermute | solution.py:344

commit v4 on v3

--- a/solution.py
+++ b/solution.py
@@ -16,6 +16,7 @@
 COLS = 8
 ROWS = 136
 LANES = 128
+VPARTS = 2
 CHUNK = 8
 CH_OUT = 4
 
@@ -77,12 +78,13 @@
 
 def shift_kernel(
     h_shift, h_weight, h_center, h_owner, h_volume, h_row, h_ref, keep, send, aux,
-    shift, weight, center, owner, volume, row_tab, rpad, sem, vsem,
+    shift, weight, center, owner, volume, row_tab, *rest,
 ):
     planes, height, width = h_volume.shape
+    rpads, sem, vsem = rest[: 2 * planes], rest[-2], rest[-1]
     tiles = width // LANES
     step = 256
-    steps = height // step
+    part = width // VPARTS
 
     def fetch(src, dst, i):
         copy = pltpu.make_async_copy(src, dst, sem.at[i])
@@ -92,10 +94,10 @@
     get_row = fetch(h_row, row_tab, 0)
     blocks = []
     for z in range(planes):
-        for n in range(steps):
-            i = z * steps + n
-            cut = pl.ds(n * step, step)
-            copy = pltpu.make_async_copy(h_volume.at[z, cut, :], volume.at[z, cut, :], vsem.at[i])
+        for n in range(VPARTS):
+            i = z * VPARTS + n
+            cut = pl.ds(n * part, part)
+            copy = pltpu.make_async_copy(h_volume.at[z, :, cut], volume.at[i], vsem.at[i])
             copy.start()
             blocks.append(copy)
             if i == 0:
@@ -107,8 +109,9 @@
 
     col = lax.axis_index("col")
     core = lax.axis_index("core")
-    rpad[:, :, :LANES] = jnp.zeros((planes, ROWS, LANES), jnp.float32)
-    rpad[:, :, LANES + width :] = jnp.zeros((planes, ROWS, LANES), jnp.float32)
+    for pad in rpads:
+        pad[:, :LANES] = jnp.zeros((ROWS, LANES), jnp.float32)
+        pad[:, LANES + width :] = jnp.zeros((ROWS, LANES), jnp.float32)
     get_center.wait()
     get_owner.wait()
     pair = lax.axis_index("line") * COLS + col
@@ -121,64 +124,90 @@
     aux[8:16, :] = jnp.sin(angle)
     who = pair * CORES + jnp.where(row == 0, core, 1 - core)
     aux[16:, :] = jnp.where(who == owner[core], 1.0, 0.0)
-
-    get_row.wait()
-    for z in range(planes):
-        for n in range(steps):
-            blocks[z * steps + n].wait()
-        for n in range(0, width, step):
-            r = dot(row_tab[...], volume[z, :, n : n + step])
-            rpad[z, :, LANES + n : LANES + n + step] = r[:ROWS] + r[ROWS:]
     get_shift.wait()
     get_weight.wait()
+    get_row.wait()
+
     lane = lax.broadcasted_iota(jnp.int32, (8, LANES), 1)
-    for t, out in ((1 - core, send), (core, keep)):
-        moves = []
-        for z in range(planes):
-            w = weight[t, z]
-            for more, factor in ((0, 1.0 - w), (1, w)):
-                s = shift[t, z] + more
-                turn = jnp.where(s < 0, s + LANES, s)
-                moves.append((z, jnp.where(s < 0, 1, 0), turn, lane < turn, factor))
+    first = lane == 0
+
+    def transform(z):
+        near = rpads[2 * z]
+        for n in range(0, width, step):
+            if n % part == 0:
+                blocks[z * VPARTS + n // part].wait()
+            at = n % part
+            r = dot(row_tab[...], volume[z * VPARTS + n // part, :, at : at + step])
+            near[:, LANES + n : LANES + n + step] = r[:ROWS] + r[ROWS:]
+
+    def move(z):
+        near, far = rpads[2 * z], rpads[2 * z + 1]
         for g in range(ROWS // 8):
             rows = slice(g * 8, g * 8 + 8)
-            total = [None] * tiles
-            for z, off, turn, mask, factor in moves:
+            turned = [pltpu.roll(near[rows, LANES * j : LANES * (j + 1)], 1, 1) for j in range(1, tiles + 1)]
+            for j in range(tiles + 1):
+                left = turned[j - 1] if j else 0.0
+                here = turned[j] if j < tiles else 0.0
+                far[rows, LANES * (j + 1) : LANES * (j + 2)] = jnp.where(first, left, here)
+        for t, out in ((1 - core, send), (core, keep)):
+            w = weight[t, z]
+            s = shift[t, z]
+            turn = jnp.where(s < 0, s + LANES, s)
+            off = jnp.where(s < 0, 1, 0)
+            mask = lane < turn
+            for g in range(ROWS // 8):
+                rows = slice(g * 8, g * 8 + 8)
                 turned = []
                 for j in range(tiles + 1):
-                    at = pl.multiple_of((j + off) * LANES, LANES)
-                    turned.append(pltpu.roll(rpad[z, rows, pl.ds(at, LANES)], turn, 1))
+                    at = pl.ds(pl.multiple_of((j + off) * LANES, LANES), LANES)
+                    mixed = (1.0 - w) * near[rows, at] + w * far[rows, at]
+                    turned.append(pltpu.roll(mixed, turn, 1))
                 for j in range(tiles):
-                    term = factor * jnp.where(mask, turned[j], turned[j + 1])
-                    total[j] = term if total[j] is None else total[j] + term
-            for j in range(tiles):
-                at = j * ROWS + g * 8
-                out[at : at + 8, :] = total[j]
+                    term = jnp.where(mask, turned[j], turned[j + 1])
+                    at = j * ROWS + g * 8
+                    out[at : at + 8, :] = term if z == 0 else out[at : at + 8, :] + term
+
+    transform(0)
+    for z in range(planes):
+        if z + 1 < planes:
+            transform(z + 1)
+        move(z)
     for copy in refs:
         copy.wait()
 
 
-def band_kernel(keep, sent, came, aux, left, share, col_tab, out, sums, lhs, proj, band, own):
+def mix_kernel(left, share, col_tab, after, out):
     width = left.shape[1]
-    tiles = width // LANES
     step = 256
     core = lax.axis_index("core")
+    at = left[pl.ds(core, 1), :]
+    w = share[pl.ds(core, 1), :]
+    near_high, near_low = halves(1.0 - w)
+    far_high, far_low = halves(w)
+    none = jnp.zeros((step, width), jnp.bfloat16)
+    x = lax.broadcasted_iota(jnp.int32, (step, width), 0).astype(jnp.float32).astype(jnp.bfloat16)
+    for n in range(0, width, step):
+
+        def is_at(place):
+            inside = (place >= 0) & (place < step)
+            return x == jnp.where(inside, place, -8).astype(jnp.float32).astype(jnp.bfloat16)
+
+        near, far = is_at(at - n), is_at(at + 1 - n)
+        high = jnp.where(near, near_high, jnp.where(far, far_high, none))
+        low = jnp.where(near, near_low, jnp.where(far, far_low, none))
+        y = dot(high, col_tab[0]) + dot(low, col_tab[0]) + dot(high, col_tab[1])
+        high, low = halves(y)
+        out[0, n : n + step, :] = high
+        out[1, n : n + step, :] = low
+
+
+def band_kernel(keep, sent, came, aux, mixed, out, sums, band, own):
+    tiles = keep.shape[0] // ROWS
     for j in range(tiles):
         rows = slice(j * ROWS, (j + 1) * ROWS)
-        sums[:ROWS, j * LANES : (j + 1) * LANES] = keep[rows, :] + came[rows, :]
-    sums[ROWS:, :] = pltpu.roll(sums[:ROWS, :], width - 1, 1)
+        sums[:, j * LANES : (j + 1) * LANES] = keep[rows, :] + came[rows, :]
     high, low = halves(sums[...])
-    lhs[: 2 * ROWS] = high
-    lhs[2 * ROWS :] = low
-    place = lax.broadcasted_iota(jnp.int32, (width, step), 0)
-    for n in range(0, width, step):
-        pick = jnp.where(place == left[pl.ds(core, 1), n : n + step], 1.0, 0.0).astype(jnp.bfloat16)
-        y = dot(lhs[...], pick)
-        y = y[: 2 * ROWS] + y[2 * ROWS :]
-        cw = share[pl.ds(core, 1), n : n + step]
-        proj[:, n : n + step] = (1.0 - cw) * y[:ROWS] + cw * y[ROWS:]
-    high, low = halves(proj[...])
-    band[...] = dot(high, col_tab[0]) + dot(low, col_tab[0]) + dot(high, col_tab[1])
+    band[...] = dot(high, mixed[0]) + dot(low, mixed[0]) + dot(high, mixed[1])
     row = band[HALF : HALF + 1, :]
     last = band[BAND : BAND + 1, :]
     band[HALF : HALF + 1, :BAND] = row[:, :BAND] + last[:, BAND:]
@@ -281,7 +310,7 @@
         row_tab = jnp.asarray(row_table(height))
         col_tab = jnp.asarray(column_table(width))
         tiles = width // LANES
-        blocks = planes * height // 256
+        blocks = planes * VPARTS
         fetched = (shift, weight, center, owner, volume, row_tab, ref)
         keep, send, aux = pl.pallas_call(
             shift_kernel,
@@ -297,9 +326,9 @@
                 pltpu.SMEM(weight.shape, f32),
                 pltpu.SMEM(center.shape, jnp.int32),
                 pltpu.SMEM(owner.shape, jnp.int32),
-                pltpu.VMEM(volume.shape, bf16),
+                pltpu.VMEM((blocks, height, width // VPARTS), bf16),
                 pltpu.VMEM(row_tab.shape, bf16),
-                pltpu.VMEM((planes, ROWS, width + 2 * LANES), f32),
+                *[pltpu.VMEM((ROWS, width + 2 * LANES), f32)] * (2 * planes),
                 pltpu.SemaphoreType.DMA((7,)),
                 pltpu.SemaphoreType.DMA((blocks,)),
             ],
@@ -307,21 +336,27 @@
             name="shift",
         )(*(pltpu.with_memory_space_constraint(a, pltpu.HBM) for a in fetched))
         came = lax.ppermute(send, "core", [(i, (i + 1) % CORES) for i in range(CORES)])
+        mixed = pl.pallas_call(
+            mix_kernel,
+            out_shape=jax.ShapeDtypeStruct(col_tab.shape, bf16),
+            in_specs=[vmem] * 4,
+            out_specs=vmem,
+            compiler_params=pltpu.CompilerParams(vmem_limit_bytes=24 * 1024 * 1024),
+            name="mix",
+        )(left, share, col_tab, aux)
         packed = pl.pallas_call(
             band_kernel,
             out_shape=jax.ShapeDtypeStruct((HALF, CHUNK, BAND), f32),
-            in_specs=[vmem] * 7,
+            in_specs=[vmem] * 5,
             out_specs=vmem,
             scratch_shapes=[
-                pltpu.VMEM((2 * ROWS, width), f32),
-                pltpu.VMEM((4 * ROWS, width), bf16),
                 pltpu.VMEM((ROWS, width), f32),
                 pltpu.VMEM((ROWS, 2 * BAND), f32),
                 pltpu.VMEM((2, BAND, BAND), f32),
             ],
             compiler_params=pltpu.CompilerParams(vmem_limit_bytes=24 * 1024 * 1024),
             name="band",
-        )(keep, send, came, aux, left, share, col_tab)
+        )(keep, send, came, aux, mixed)
         got = lax.all_to_all(packed, ("line", "col"), 0, 0, tiled=True)
         piece = pl.pallas_call(
             cross_kernel,

time: 69.6 us -> 67.5 us (0.970)
  waiting for transfers between devices: 2.59 us -> 0.82 us
    pallas_call x0 -> x1, Pallas kernels: none -> 1.82 us  [per_device(): pl.pallas_call(mix_kernel, out_shape=jax.ShapeDtypeStruct(col_tab.shape,...]
    ppermute x2, waiting for transfers between devices: 2.59 us -> 0.82 us  [per_device(): lax.ppermute(send, 'core', [(i, (i + 1) % CORES) for i in range(CORES)])]
    pallas_call x1, Pallas kernels: 2.21 us -> 0.6 us  [per_device(): pl.pallas_call(band_kernel, out_shape=jax.ShapeDtypeStruct((HALF, CHUNK,...]
  transfers between devices with their start and end apart: 2 -> 2, of which waited for: 2 -> 1; matrix products, arithmetic and copies ran while one was open for 0% -> 0% of each run, Pallas kernels for 0% -> 3%
where the time goes in v4:
time: 67.5 us; the launch traced here: 67.3 us
  blocking collectives  34.7 us (51%)
  starting transfers between devices  23.3 us (35%)
  Pallas kernels  7.83 us (12%)
  waiting for transfers between devices  0.82 us (1%)
  between operations  0.72 us (1%)
    ppermute x2, starting transfers between devices, per_device(): lax.ppermute(send, 'core', [(i, (i + 1) % CORES) for i in range(CORES)])  23.3 us
    all_to_all x1, blocking collectives, per_device(): got = lax.all_to_all(packed, ('line', 'col'), 0, 0, tiled=True)  17.7 us
    all_to_all x1, blocking collectives, per_device(): got = lax.all_to_all(piece, ('line', 'col'), 0, 0, tiled=True)  16.9 us
    pallas_call x1, Pallas kernels, per_device(): pl.pallas_call(shift_kernel, out_shape=[jax.ShapeDtypeStruct((tiles * ROW...  4.24 us
    pallas_call x1, Pallas kernels, per_device(): pl.pallas_call(mix_kernel, out_shape=jax.ShapeDtypeStruct(col_tab.shape,...  1.82 us
  transfers between devices with their start and end apart: 2, of which 1 were waited for; matrix products, arithmetic and copies ran while one was open for 0% of the time, Pallas kernels for 3%

profile of v4, /device:TPU:513, one launch (start us, length us, event | category | flops | bytes accessed | tf_op | source)
XLA Modules:
  0.0 67.3 jit_solution(17350102754057351818)
XLA Ops:
  0.6 0.0 copy-start
  0.6 0.0 copy-start.2
  0.7 0.0 copy-start.4
  0.7 0.0 copy-start.3
  0.7 4.2 %shift.1 = (f32[1088,128]{1,0:T(8,128)S(1)}, f32[1344,128]{1,0:T(8,128)S(1)}, f32[24,128]{1,0:T(8,128)S(1)}) custom-call(s32[2,2]{1,0:T(2,128)} %h_shift.1, f32[2,2]{1,0:T(2,128)} %h_weight.1, s32[2,2]{1,0:T(2,128)} %h_center.1, s32[128]{0:T(128)} %h_owner.1, bf16[2,1024,1024]{2,1,0:T(8,128)(2,1)} %h_volume.1, bf16[272,1024]{1,0:T(8,128)(2,1)} %constant.8.clone.h_row, ...), custom_call_target="tpu_custom_call" | custom-call | tf_op jit(solution)/shard_map/shift/pallas_call | solution.py:315
  4.9 0.0 copy-start.1
  4.9 20.5 %collective-permute-start = (f32[1344,128]{1,0:T(8,128)S(1)}, f32[1344,128]{1,0:T(8,128)S(1)}, u32[]{:S(2)}, u32[]{:S(2)}) collective-permute-start(f32[1344,128]{1,0:T(8,128)S(1)} %get-tuple-element.9.sent), channel_id=1, source_target_pairs={{0,1},{1,0},{2,3},{3,2},{4,5},{5,4},{6,7},{7,6},{8,9},{9,8},{10,11... | collective-permute-start | bytes 2064392 | tf_op jit(solution)/shard_map/ppermute | solution.py:338
  25.5 0.0 copy-done
  25.5 0.0 copy-done.4
  25.5 0.0 copy-done.3
  25.5 1.8 %mix.1.mixed = bf16[2,1024,256]{2,1,0:T(8,128)(2,1)S(1)} custom-call(s32[2,1024]{1,0:T(2,128)S(1)} %copy-done.3, f32[2,1024]{1,0:T(2,128)S(1)} %copy-done.4, bf16[2,1024,256]{2,1,0:T(8,128)(2,1)S(1)} %copy-done, f32[24,128]{1,0:T(8,128)S(1)} %get-tuple-element.7.after.aux), custom_call_target="tpu_custom_call" | custom-call | tf_op jit(solution)/shard_map/mix/pallas_call | solution.py:339
  27.3 0.0 collective-permute-done.came
  27.3 0.6 band.1
  27.9 17.7 %all_to_all.10.got = f32[64,8,128]{2,1,0:T(8,128)S(1)} all-to-all(f32[64,8,128]{2,1,0:T(8,128)S(1)} %band.1), channel_id=1, replica_groups=mesh['grp'=2,'line'=8,'col'=8,'core'=2] {'line','col'}, dimensions={0} | all-to-all | bytes 524288 | tf_op jit(solution)/shard_map/all_to_all | solution.py:360
  45.6 0.0 copy-done.2
  45.6 0.2 cross.1
  45.9 16.9 %all_to_all.11.got = f32[64,4,128]{2,1,0:T(4,128)S(1)} all-to-all(f32[64,4,128]{2,1,0:T(4,128)S(1)} %cross.1), channel_id=1, replica_groups=mesh['grp'=2,'line'=8,'col'=8,'core'=2] {'line','col'}, dimensions={0} | all-to-all | bytes 262144 | tf_op jit(solution)/shard_map/all_to_all | solution.py:370
  62.8 0.0 copy-done.1
  62.8 0.3 window.1
  63.1 2.7 %collective-permute-start.1 = (f32[2,128]{1,0:T(2,128)S(1)}, f32[2,128]{1,0:T(2,128)S(1)}, u32[]{:S(2)}, u32[]{:S(2)}) collective-permute-start(f32[2,128]{1,0:T(2,128)S(1)} %get-tuple-element.11), channel_id=1, source_target_pairs={{0,1},{1,0},{2,3},{3,2},{4,5},{5,4},{6,7},{7,6},{8,9},{9,8},{10,11... | collective-permute-start | bytes 3080 | tf_op jit(solution)/shard_map/ppermute | solution.py:379
  65.9 0.8 %collective-permute-done.1.came = f32[2,128]{1,0:T(2,128)S(1)} collective-permute-done((f32[2,128]{1,0:T(2,128)S(1)}, f32[2,128]{1,0:T(2,128)S(1)}, u32[]{:S(2)}, u32[]{:S(2)}) %collective-permute-start.1) | collective-permute-done | bytes 1056 | tf_op jit(solution)/shard_map/ppermute | solution.py:379
  66.7 0.6 join.1
Async XLA Ops:
  0.6 24.8 %copy-start = (bf16[2,1024,256]{2,1,0:T(8,128)(2,1)S(1)}, bf16[2,1024,256]{2,1,0:T(8,128)(2,1)}, u32[]{:S(2)}) copy-start(bf16[2,1024,256]{2,1,0:T(8,128)(2,1)} %constant.9.clone.col_tab) | copy-start | bytes 3145732
  0.6 45.0 %copy-start.2 = (bf16[2,256,128]{2,1,0:T(8,128)(2,1)S(1)}, bf16[2,256,128]{2,1,0:T(8,128)(2,1)}, u32[]{:S(2)}) copy-start(bf16[2,256,128]{2,1,0:T(8,128)(2,1)} %constant.10.clone.tab) | copy-start | bytes 393220
  0.7 24.8 %copy-start.4 = (f32[2,1024]{1,0:T(2,128)S(1)}, f32[2,1024]{1,0:T(2,128)}, u32[]{:S(2)}) copy-start(f32[2,1024]{1,0:T(2,128)} %share.1) | copy-start | bytes 24580
  0.7 24.8 %copy-start.3 = (s32[2,1024]{1,0:T(2,128)S(1)}, s32[2,1024]{1,0:T(2,128)}, u32[]{:S(2)}) copy-start(s32[2,1024]{1,0:T(2,128)} %left.1) | copy-start | bytes 24580
  4.9 57.9 %copy-start.1 = (bf16[2,128,256]{2,1,0:T(8,128)(2,1)S(1)}, bf16[2,128,256]{2,1,0:T(8,128)(2,1)}, u32[]{:S(2)}) copy-start(bf16[2,128,256]{2,1,0:T(8,128)(2,1)} %constant.11.clone.tab) | copy-start | bytes 393220
  4.9 22.4 %collective-permute-start = (f32[1344,128]{1,0:T(8,128)S(1)}, f32[1344,128]{1,0:T(8,128)S(1)}, u32[]{:S(2)}, u32[]{:S(2)}) collective-permute-start(f32[1344,128]{1,0:T(8,128)S(1)} %get-tuple-element.9.sent), channel_id=1, source_target_pairs={{0,1},{1,0},{2,3},{3,2},{4,5},{5,4},{6,7},{7,6},{8,9},{9,8},{10,11... | collective-permute-start | bytes 2064392 | tf_op jit(solution)/shard_map/ppermute | solution.py:338
  63.1 3.5 %collective-permute-start.1 = (f32[2,128]{1,0:T(2,128)S(1)}, f32[2,128]{1,0:T(2,128)S(1)}, u32[]{:S(2)}, u32[]{:S(2)}) collective-permute-start(f32[2,128]{1,0:T(2,128)S(1)} %get-tuple-element.11), channel_id=1, source_target_pairs={{0,1},{1,0},{2,3},{3,2},{4,5},{5,4},{6,7},{7,6},{8,9},{9,8},{10,11... | collective-permute-start | bytes 3080 | tf_op jit(solution)/shard_map/ppermute | solution.py:379

commit v5 on v4

--- a/solution.py
+++ b/solution.py
@@ -84,7 +84,7 @@
     rpads, sem, vsem = rest[: 2 * planes], rest[-2], rest[-1]
     tiles = width // LANES
     step = 256
-    part = width // VPARTS
+    part = height // VPARTS
 
     def fetch(src, dst, i):
         copy = pltpu.make_async_copy(src, dst, sem.at[i])
@@ -97,7 +97,7 @@
         for n in range(VPARTS):
             i = z * VPARTS + n
             cut = pl.ds(n * part, part)
-            copy = pltpu.make_async_copy(h_volume.at[z, :, cut], volume.at[i], vsem.at[i])
+            copy = pltpu.make_async_copy(h_volume.at[z, cut, :], volume.at[z, cut, :], vsem.at[i])
             copy.start()
             blocks.append(copy)
             if i == 0:
@@ -109,9 +109,6 @@
 
     col = lax.axis_index("col")
     core = lax.axis_index("core")
-    for pad in rpads:
-        pad[:, :LANES] = jnp.zeros((ROWS, LANES), jnp.float32)
-        pad[:, LANES + width :] = jnp.zeros((ROWS, LANES), jnp.float32)
     get_center.wait()
     get_owner.wait()
     pair = lax.axis_index("line") * COLS + col
@@ -133,37 +130,39 @@
 
     def transform(z):
         near = rpads[2 * z]
+        for copy in blocks[z * VPARTS : (z + 1) * VPARTS]:
+            copy.wait()
         for n in range(0, width, step):
-            if n % part == 0:
-                blocks[z * VPARTS + n // part].wait()
-            at = n % part
-            r = dot(row_tab[...], volume[z * VPARTS + n // part, :, at : at + step])
-            near[:, LANES + n : LANES + n + step] = r[:ROWS] + r[ROWS:]
+            r = dot(row_tab[...], volume[z, :, n : n + step])
+            near[:, n : n + step] = r[:ROWS] + r[ROWS:]
 
     def move(z):
         near, far = rpads[2 * z], rpads[2 * z + 1]
         for g in range(ROWS // 8):
             rows = slice(g * 8, g * 8 + 8)
-            turned = [pltpu.roll(near[rows, LANES * j : LANES * (j + 1)], 1, 1) for j in range(1, tiles + 1)]
+            turned = [pltpu.roll(near[rows, LANES * j : LANES * (j + 1)], 1, 1) for j in range(tiles)]
             for j in range(tiles + 1):
                 left = turned[j - 1] if j else 0.0
                 here = turned[j] if j < tiles else 0.0
-                far[rows, LANES * (j + 1) : LANES * (j + 2)] = jnp.where(first, left, here)
+                far[rows, LANES * j : LANES * (j + 1)] = jnp.where(first, left, here)
         for t, out in ((1 - core, send), (core, keep)):
             w = weight[t, z]
             s = shift[t, z]
             turn = jnp.where(s < 0, s + LANES, s)
-            off = jnp.where(s < 0, 1, 0)
-            mask = lane < turn
+            before = lane < jnp.where(s < 0, 0, s)
+            after = lane >= jnp.where(s < 0, s + LANES, LANES)
             for g in range(ROWS // 8):
                 rows = slice(g * 8, g * 8 + 8)
                 turned = []
                 for j in range(tiles + 1):
-                    at = pl.ds(pl.multiple_of((j + off) * LANES, LANES), LANES)
-                    mixed = (1.0 - w) * near[rows, at] + w * far[rows, at]
+                    at = slice(LANES * j, LANES * (j + 1))
+                    mixed = w * far[rows, at]
+                    if j < tiles:
+                        mixed = (1.0 - w) * near[rows, at] + mixed
                     turned.append(pltpu.roll(mixed, turn, 1))
                 for j in range(tiles):
-                    term = jnp.where(mask, turned[j], turned[j + 1])
+                    left = turned[j - 1] if j else 0.0
+                    term = jnp.where(before, left, jnp.where(after, turned[j + 1], turned[j]))
                     at = j * ROWS + g * 8
                     out[at : at + 8, :] = term if z == 0 else out[at : at + 8, :] + term
 
@@ -326,9 +325,9 @@
                 pltpu.SMEM(weight.shape, f32),
                 pltpu.SMEM(center.shape, jnp.int32),
                 pltpu.SMEM(owner.shape, jnp.int32),
-                pltpu.VMEM((blocks, height, width // VPARTS), bf16),
+                pltpu.VMEM(volume.shape, bf16),
                 pltpu.VMEM(row_tab.shape, bf16),
-                *[pltpu.VMEM((ROWS, width + 2 * LANES), f32)] * (2 * planes),
+                *[pltpu.VMEM((ROWS, width + LANES), f32)] * (2 * planes),
                 pltpu.SemaphoreType.DMA((7,)),
                 pltpu.SemaphoreType.DMA((blocks,)),
             ],

time: 67.5 us -> 67.1 us (level)
  no operation moved by 1% of the time
where the time goes in v5:
time: 67.1 us; the launch traced here: 66.9 us
  blocking collectives  34.6 us (52%)
  starting transfers between devices  23.3 us (35%)
  Pallas kernels  7.37 us (11%)
  waiting for transfers between devices  0.82 us (1%)
  between operations  0.72 us (1%)
    ppermute x2, starting transfers between devices, per_device(): lax.ppermute(send, 'core', [(i, (i + 1) % CORES) for i in range(CORES)])  23.3 us
    all_to_all x1, blocking collectives, per_device(): got = lax.all_to_all(packed, ('line', 'col'), 0, 0, tiled=True)  17.7 us
    all_to_all x1, blocking collectives, per_device(): got = lax.all_to_all(piece, ('line', 'col'), 0, 0, tiled=True)  16.9 us
    pallas_call x1, Pallas kernels, per_device(): pl.pallas_call(shift_kernel, out_shape=[jax.ShapeDtypeStruct((tiles * ROW...  3.79 us
    pallas_call x1, Pallas kernels, per_device(): pl.pallas_call(mix_kernel, out_shape=jax.ShapeDtypeStruct(col_tab.shape,...  1.81 us
  transfers between devices with their start and end apart: 2, of which 1 were waited for; matrix products, arithmetic and copies ran while one was open for 0% of the time, Pallas kernels for 3%

profile of v5, /device:TPU:513, one launch (start us, length us, event | category | flops | bytes accessed | tf_op | source)
XLA Modules:
  0.0 66.9 jit_solution(8079009931625508301)
XLA Ops:
  0.6 0.0 copy-start
  0.6 0.0 copy-start.2
  0.7 0.0 copy-start.4
  0.7 0.0 copy-start.3
  0.7 3.8 %shift.1 = (f32[1088,128]{1,0:T(8,128)S(1)}, f32[1344,128]{1,0:T(8,128)S(1)}, f32[24,128]{1,0:T(8,128)S(1)}) custom-call(s32[2,2]{1,0:T(2,128)} %h_shift.1, f32[2,2]{1,0:T(2,128)} %h_weight.1, s32[2,2]{1,0:T(2,128)} %h_center.1, s32[128]{0:T(128)} %h_owner.1, bf16[2,1024,1024]{2,1,0:T(8,128)(2,1)} %h_volume.1, bf16[272,1024]{1,0:T(8,128)(2,1)} %constant.8.clone.h_row, ...), custom_call_target="tpu_custom_call" | custom-call | tf_op jit(solution)/shard_map/shift/pallas_call | solution.py:314
  4.5 0.0 copy-start.1
  4.5 20.5 %collective-permute-start = (f32[1344,128]{1,0:T(8,128)S(1)}, f32[1344,128]{1,0:T(8,128)S(1)}, u32[]{:S(2)}, u32[]{:S(2)}) collective-permute-start(f32[1344,128]{1,0:T(8,128)S(1)} %get-tuple-element.9.sent), channel_id=1, source_target_pairs={{0,1},{1,0},{2,3},{3,2},{4,5},{5,4},{6,7},{7,6},{8,9},{9,8},{10,11... | collective-permute-start | bytes 2064392 | tf_op jit(solution)/shard_map/ppermute | solution.py:337
  25.0 0.0 copy-done
  25.0 0.0 copy-done.4
  25.0 0.0 copy-done.3
  25.0 1.8 %mix.1.mixed = bf16[2,1024,256]{2,1,0:T(8,128)(2,1)S(1)} custom-call(s32[2,1024]{1,0:T(2,128)S(1)} %copy-done.3, f32[2,1024]{1,0:T(2,128)S(1)} %copy-done.4, bf16[2,1024,256]{2,1,0:T(8,128)(2,1)S(1)} %copy-done, f32[24,128]{1,0:T(8,128)S(1)} %get-tuple-element.7.after.aux), custom_call_target="tpu_custom_call" | custom-call | tf_op jit(solution)/shard_map/mix/pallas_call | solution.py:338
  26.8 0.0 collective-permute-done.came
  26.9 0.6 band.1
  27.5 17.7 %all_to_all.10.got = f32[64,8,128]{2,1,0:T(8,128)S(1)} all-to-all(f32[64,8,128]{2,1,0:T(8,128)S(1)} %band.1), channel_id=1, replica_groups=mesh['grp'=2,'line'=8,'col'=8,'core'=2] {'line','col'}, dimensions={0} | all-to-all | bytes 524288 | tf_op jit(solution)/shard_map/all_to_all | solution.py:359
  45.2 0.0 copy-done.2
  45.2 0.2 cross.1
  45.4 16.9 %all_to_all.11.got = f32[64,4,128]{2,1,0:T(4,128)S(1)} all-to-all(f32[64,4,128]{2,1,0:T(4,128)S(1)} %cross.1), channel_id=1, replica_groups=mesh['grp'=2,'line'=8,'col'=8,'core'=2] {'line','col'}, dimensions={0} | all-to-all | bytes 262144 | tf_op jit(solution)/shard_map/all_to_all | solution.py:369
  62.3 0.0 copy-done.1
  62.3 0.3 window.1
  62.7 2.8 %collective-permute-start.1 = (f32[2,128]{1,0:T(2,128)S(1)}, f32[2,128]{1,0:T(2,128)S(1)}, u32[]{:S(2)}, u32[]{:S(2)}) collective-permute-start(f32[2,128]{1,0:T(2,128)S(1)} %get-tuple-element.11), channel_id=1, source_target_pairs={{0,1},{1,0},{2,3},{3,2},{4,5},{5,4},{6,7},{7,6},{8,9},{9,8},{10,11... | collective-permute-start | bytes 3080 | tf_op jit(solution)/shard_map/ppermute | solution.py:378
  65.4 0.8 %collective-permute-done.1.came = f32[2,128]{1,0:T(2,128)S(1)} collective-permute-done((f32[2,128]{1,0:T(2,128)S(1)}, f32[2,128]{1,0:T(2,128)S(1)}, u32[]{:S(2)}, u32[]{:S(2)}) %collective-permute-start.1) | collective-permute-done | bytes 1056 | tf_op jit(solution)/shard_map/ppermute | solution.py:378
  66.2 0.6 join.1
Async XLA Ops:
  0.6 24.4 %copy-start = (bf16[2,1024,256]{2,1,0:T(8,128)(2,1)S(1)}, bf16[2,1024,256]{2,1,0:T(8,128)(2,1)}, u32[]{:S(2)}) copy-start(bf16[2,1024,256]{2,1,0:T(8,128)(2,1)} %constant.9.clone.col_tab) | copy-start | bytes 3145732
  0.6 44.5 %copy-start.2 = (bf16[2,256,128]{2,1,0:T(8,128)(2,1)S(1)}, bf16[2,256,128]{2,1,0:T(8,128)(2,1)}, u32[]{:S(2)}) copy-start(bf16[2,256,128]{2,1,0:T(8,128)(2,1)} %constant.10.clone.tab) | copy-start | bytes 393220
  0.7 24.4 %copy-start.4 = (f32[2,1024]{1,0:T(2,128)S(1)}, f32[2,1024]{1,0:T(2,128)}, u32[]{:S(2)}) copy-start(f32[2,1024]{1,0:T(2,128)} %share.1) | copy-start | bytes 24580
  0.7 24.4 %copy-start.3 = (s32[2,1024]{1,0:T(2,128)S(1)}, s32[2,1024]{1,0:T(2,128)}, u32[]{:S(2)}) copy-start(s32[2,1024]{1,0:T(2,128)} %left.1) | copy-start | bytes 24580
  4.5 57.8 %copy-start.1 = (bf16[2,128,256]{2,1,0:T(8,128)(2,1)S(1)}, bf16[2,128,256]{2,1,0:T(8,128)(2,1)}, u32[]{:S(2)}) copy-start(bf16[2,128,256]{2,1,0:T(8,128)(2,1)} %constant.11.clone.tab) | copy-start | bytes 393220
  4.5 22.4 %collective-permute-start = (f32[1344,128]{1,0:T(8,128)S(1)}, f32[1344,128]{1,0:T(8,128)S(1)}, u32[]{:S(2)}, u32[]{:S(2)}) collective-permute-start(f32[1344,128]{1,0:T(8,128)S(1)} %get-tuple-element.9.sent), channel_id=1, source_target_pairs={{0,1},{1,0},{2,3},{3,2},{4,5},{5,4},{6,7},{7,6},{8,9},{9,8},{10,11... | collective-permute-start | bytes 2064392 | tf_op jit(solution)/shard_map/ppermute | solution.py:337
  62.7 3.6 %collective-permute-start.1 = (f32[2,128]{1,0:T(2,128)S(1)}, f32[2,128]{1,0:T(2,128)S(1)}, u32[]{:S(2)}, u32[]{:S(2)}) collective-permute-start(f32[2,128]{1,0:T(2,128)S(1)} %get-tuple-element.11), channel_id=1, source_target_pairs={{0,1},{1,0},{2,3},{3,2},{4,5},{5,4},{6,7},{7,6},{8,9},{9,8},{10,11... | collective-permute-start | bytes 3080 | tf_op jit(solution)/shard_map/ppermute | solution.py:378

commit v6 on v5

--- a/solution.py
+++ b/solution.py
@@ -130,11 +130,19 @@
 
     def transform(z):
         near = rpads[2 * z]
-        for copy in blocks[z * VPARTS : (z + 1) * VPARTS]:
-            copy.wait()
-        for n in range(0, width, step):
-            r = dot(row_tab[...], volume[z, :, n : n + step])
-            near[:, n : n + step] = r[:ROWS] + r[ROWS:]
+        mine = blocks[z * VPARTS : (z + 1) * VPARTS]
+        cuts = [slice(n * part, (n + 1) * part) for n in range(VPARTS)]
+        if z:
+            for copy in mine:
+                copy.wait()
+            cuts = [slice(0, height)]
+        for i, cut in enumerate(cuts):
+            if not z:
+                mine[i].wait()
+            for n in range(0, width, step):
+                r = dot(row_tab[:, cut], volume[z, cut, n : n + step])
+                r = r[:ROWS] + r[ROWS:]
+                near[:, n : n + step] = near[:, n : n + step] + r if i else r
 
     def move(z):
         near, far = rpads[2 * z], rpads[2 * z + 1]
@@ -288,8 +296,8 @@
     core = lax.axis_index("core")
     rows[pl.ds(core, 1), 0, :] = keep[0:1, :]
     rows[pl.ds(1 - core, 1), 0, :] = came[0:1, :]
-    peaks[core] = jnp.max(keep[1:2, :])
-    peaks[1 - core] = jnp.max(came[1:2, :])
+    peaks[core] = keep[1, 0]
+    peaks[1 - core] = came[1, 0]
 
 
 def solution(mesh):

time: 67.1 us -> 66.9 us (level)
  no operation moved by 1% of the time
where the time goes in v6:
time: 66.9 us; the launch traced here: 66.7 us
  blocking collectives  34.7 us (52%)
  starting transfers between devices  23.3 us (35%)
  Pallas kernels  7.23 us (11%)
  waiting for transfers between devices  0.82 us (1%)
  between operations  0.72 us (1%)
    ppermute x2, starting transfers between devices, per_device(): lax.ppermute(send, 'core', [(i, (i + 1) % CORES) for i in range(CORES)])  23.3 us
    all_to_all x1, blocking collectives, per_device(): got = lax.all_to_all(packed, ('line', 'col'), 0, 0, tiled=True)  17.7 us
    all_to_all x1, blocking collectives, per_device(): got = lax.all_to_all(piece, ('line', 'col'), 0, 0, tiled=True)  16.9 us
    pallas_call x1, Pallas kernels, per_device(): pl.pallas_call(shift_kernel, out_shape=[jax.ShapeDtypeStruct((tiles * ROW...  3.7 us
    pallas_call x1, Pallas kernels, per_device(): pl.pallas_call(mix_kernel, out_shape=jax.ShapeDtypeStruct(col_tab.shape,...  1.82 us
  transfers between devices with their start and end apart: 2, of which 1 were waited for; matrix products, arithmetic and copies ran while one was open for 0% of the time, Pallas kernels for 3%

profile of v6, /device:TPU:513, one launch (start us, length us, event | category | flops | bytes accessed | tf_op | source)
XLA Modules:
  0.0 66.7 jit_solution(18253925046618262285)
XLA Ops:
  0.6 0.0 copy-start
  0.6 0.0 copy-start.2
  0.7 0.0 copy-start.4
  0.7 0.0 copy-start.3
  0.7 3.7 %shift.1 = (f32[1088,128]{1,0:T(8,128)S(1)}, f32[1344,128]{1,0:T(8,128)S(1)}, f32[24,128]{1,0:T(8,128)S(1)}) custom-call(s32[2,2]{1,0:T(2,128)} %h_shift.1, f32[2,2]{1,0:T(2,128)} %h_weight.1, s32[2,2]{1,0:T(2,128)} %h_center.1, s32[128]{0:T(128)} %h_owner.1, bf16[2,1024,1024]{2,1,0:T(8,128)(2,1)} %h_volume.1, bf16[272,1024]{1,0:T(8,128)(2,1)} %constant.8.clone.h_row, ...), custom_call_target="tpu_custom_call" | custom-call | tf_op jit(solution)/shard_map/shift/pallas_call | solution.py:322
  4.4 0.0 copy-start.1
  4.4 20.5 %collective-permute-start = (f32[1344,128]{1,0:T(8,128)S(1)}, f32[1344,128]{1,0:T(8,128)S(1)}, u32[]{:S(2)}, u32[]{:S(2)}) collective-permute-start(f32[1344,128]{1,0:T(8,128)S(1)} %get-tuple-element.9.sent), channel_id=1, source_target_pairs={{0,1},{1,0},{2,3},{3,2},{4,5},{5,4},{6,7},{7,6},{8,9},{9,8},{10,11... | collective-permute-start | bytes 2064392 | tf_op jit(solution)/shard_map/ppermute | solution.py:345
  24.9 0.0 copy-done
  24.9 0.0 copy-done.4
  24.9 0.0 copy-done.3
  24.9 1.8 %mix.1.mixed = bf16[2,1024,256]{2,1,0:T(8,128)(2,1)S(1)} custom-call(s32[2,1024]{1,0:T(2,128)S(1)} %copy-done.3, f32[2,1024]{1,0:T(2,128)S(1)} %copy-done.4, bf16[2,1024,256]{2,1,0:T(8,128)(2,1)S(1)} %copy-done, f32[24,128]{1,0:T(8,128)S(1)} %get-tuple-element.7.after.aux), custom_call_target="tpu_custom_call" | custom-call | tf_op jit(solution)/shard_map/mix/pallas_call | solution.py:346
  26.8 0.0 collective-permute-done.came
  26.8 0.6 band.1
  27.4 17.7 %all_to_all.10.got = f32[64,8,128]{2,1,0:T(8,128)S(1)} all-to-all(f32[64,8,128]{2,1,0:T(8,128)S(1)} %band.1), channel_id=1, replica_groups=mesh['grp'=2,'line'=8,'col'=8,'core'=2] {'line','col'}, dimensions={0} | all-to-all | bytes 524288 | tf_op jit(solution)/shard_map/all_to_all | solution.py:367
  45.1 0.0 copy-done.2
  45.1 0.2 cross.1
  45.3 16.9 %all_to_all.11.got = f32[64,4,128]{2,1,0:T(4,128)S(1)} all-to-all(f32[64,4,128]{2,1,0:T(4,128)S(1)} %cross.1), channel_id=1, replica_groups=mesh['grp'=2,'line'=8,'col'=8,'core'=2] {'line','col'}, dimensions={0} | all-to-all | bytes 262144 | tf_op jit(solution)/shard_map/all_to_all | solution.py:377
  62.3 0.0 copy-done.1
  62.3 0.3 window.1
  62.6 2.7 %collective-permute-start.1 = (f32[2,128]{1,0:T(2,128)S(1)}, f32[2,128]{1,0:T(2,128)S(1)}, u32[]{:S(2)}, u32[]{:S(2)}) collective-permute-start(f32[2,128]{1,0:T(2,128)S(1)} %get-tuple-element.11), channel_id=1, source_target_pairs={{0,1},{1,0},{2,3},{3,2},{4,5},{5,4},{6,7},{7,6},{8,9},{9,8},{10,11... | collective-permute-start | bytes 3080 | tf_op jit(solution)/shard_map/ppermute | solution.py:386
  65.3 0.8 %collective-permute-done.1.came = f32[2,128]{1,0:T(2,128)S(1)} collective-permute-done((f32[2,128]{1,0:T(2,128)S(1)}, f32[2,128]{1,0:T(2,128)S(1)}, u32[]{:S(2)}, u32[]{:S(2)}) %collective-permute-start.1) | collective-permute-done | bytes 1056 | tf_op jit(solution)/shard_map/ppermute | solution.py:386
  66.2 0.6 join.1
Async XLA Ops:
  0.6 24.3 %copy-start = (bf16[2,1024,256]{2,1,0:T(8,128)(2,1)S(1)}, bf16[2,1024,256]{2,1,0:T(8,128)(2,1)}, u32[]{:S(2)}) copy-start(bf16[2,1024,256]{2,1,0:T(8,128)(2,1)} %constant.9.clone.col_tab) | copy-start | bytes 3145732
  0.6 44.5 %copy-start.2 = (bf16[2,256,128]{2,1,0:T(8,128)(2,1)S(1)}, bf16[2,256,128]{2,1,0:T(8,128)(2,1)}, u32[]{:S(2)}) copy-start(bf16[2,256,128]{2,1,0:T(8,128)(2,1)} %constant.10.clone.tab) | copy-start | bytes 393220
  0.7 24.3 %copy-start.4 = (f32[2,1024]{1,0:T(2,128)S(1)}, f32[2,1024]{1,0:T(2,128)}, u32[]{:S(2)}) copy-start(f32[2,1024]{1,0:T(2,128)} %share.1) | copy-start | bytes 24580
  0.7 24.3 %copy-start.3 = (s32[2,1024]{1,0:T(2,128)S(1)}, s32[2,1024]{1,0:T(2,128)}, u32[]{:S(2)}) copy-start(s32[2,1024]{1,0:T(2,128)} %left.1) | copy-start | bytes 24580
  4.4 57.9 %copy-start.1 = (bf16[2,128,256]{2,1,0:T(8,128)(2,1)S(1)}, bf16[2,128,256]{2,1,0:T(8,128)(2,1)}, u32[]{:S(2)}) copy-start(bf16[2,128,256]{2,1,0:T(8,128)(2,1)} %constant.11.clone.tab) | copy-start | bytes 393220
  4.4 22.4 %collective-permute-start = (f32[1344,128]{1,0:T(8,128)S(1)}, f32[1344,128]{1,0:T(8,128)S(1)}, u32[]{:S(2)}, u32[]{:S(2)}) collective-permute-start(f32[1344,128]{1,0:T(8,128)S(1)} %get-tuple-element.9.sent), channel_id=1, source_target_pairs={{0,1},{1,0},{2,3},{3,2},{4,5},{5,4},{6,7},{7,6},{8,9},{9,8},{10,11... | collective-permute-start | bytes 2064392 | tf_op jit(solution)/shard_map/ppermute | solution.py:345
  62.6 3.5 %collective-permute-start.1 = (f32[2,128]{1,0:T(2,128)S(1)}, f32[2,128]{1,0:T(2,128)S(1)}, u32[]{:S(2)}, u32[]{:S(2)}) collective-permute-start(f32[2,128]{1,0:T(2,128)S(1)} %get-tuple-element.11), channel_id=1, source_target_pairs={{0,1},{1,0},{2,3},{3,2},{4,5},{5,4},{6,7},{7,6},{8,9},{9,8},{10,11... | collective-permute-start | bytes 3080 | tf_op jit(solution)/shard_map/ppermute | solution.py:386
